TPU v7x, 32 devices: a whole 2x2x4 slice. The times are simulated.
32 devices in a mesh: grid: 4 (over z), line: 8 (over y, x, core).
Axes of the slice: x: 2, y: 2, z: 4, core: 2. Of those that a mesh axis runs over, the one named last changes fastest.
Arguments:
- les: float32 [24, 4, 1024], P(None, 'grid', 'line'), may hold values from -6 to 6
- lines: float32 [4, 8, 128, 24, 128], P('grid', 'line'), may hold values from -6 to 6
- triplet_start: int32 [2, 4, 8, 128], P(None, 'grid', 'line'), may hold values from 0 to 80
- splice_owner: int32 [2, 4, 8, 128, 1], P(None, 'grid', 'line'), may hold values from 0 to 31; in each aligned block of 128 rows (0 to 127, 128 to 255, ..., all dimensions but the last counted through in order) at most 8 rows name the same one
- splice_line: int32 [2, 4, 8, 128], P(None, 'grid', 'line'), may hold values from 0 to 127
- splice_from: int32 [2, 4, 8, 128], P(None, 'grid', 'line'), may hold values from 0 to 7
- splice_to: int32 [2, 4, 8, 128], P(None, 'grid', 'line'), may hold values from 0 to 7
- chem_counts: int32 [4, 8, 128], P('grid', 'line'), may hold values from 1 to 6, as said below
- diffusivity: float32 [24], replicated, may hold values from 0.5 to 20
- rates: float32 [24, 24], replicated, may hold values from -1.25 to 1.25
- frozen_inverse: float32 [24, 24], replicated, may hold values from -0.3 to 0.5
Outputs:
- les_out: float32 [24, 4, 1024], P(None, 'grid', 'line')
- lines_out: float32 [4, 8, 128, 24, 128], P('grid', 'line')
Inputs may be any that keep to these rules, and one draw needn't show every extreme that they name: `splice_owner`: in the rows of one device and one step no owner is named more than 8 times, a bound that some block reaches. `chem_counts`: some line has 6 substeps.
All inputs are finite; a program needn't handle non-finite values.
Results may differ from a plain program's by a relative error of at most 0.0003.
Values sent between devices are 32-bit elements; how exact they have to be, the bound alone decides.
A program may use at most 64 MiB of HBM per device.

v0:
```python
import jax
import jax.numpy as jnp
from jax import lax
from jax.sharding import PartitionSpec as P

SEG = 16
TRIP = 48
STEPS = 2


les_rate = 0.2
relax_rate = 0.5
splice_weight = 0.5


def padded_2(array, sides, width):
    for axis, dim in sides:
        peers, length = (lax.axis_size(axis), array.shape[dim])
        up = [(i, (i + 1) % peers) for i in range(peers - 1)]
        down = [(j, i) for i, j in up]
        last = lax.slice_in_dim(array, length - width, length, axis=dim)
        leading = lax.slice_in_dim(array, 0, width, axis=dim)
        before = lax.ppermute(last, axis, up)
        after = lax.ppermute(leading, axis, down)
        array = jnp.concatenate([before, array, after], axis=dim)
    return array


def diffusion_inverse(diffusivity, points):
    place = jnp.arange(points)
    ends = ((place == 0) | (place == points - 1)).astype(jnp.float32)
    coeff = diffusivity[:, None]
    main = 1.0 + coeff * (2.0 - ends[None, :])
    off_diag = -coeff * jnp.ones((1, points), jnp.float32)
    lower = jnp.where(place[None, :] == 0, jnp.float32(0.0), off_diag)
    upper = jnp.where(place[None, :] == points - 1, jnp.float32(0.0), off_diag)
    ident = jnp.broadcast_to(
        jnp.eye(points, dtype=jnp.float32), (diffusivity.shape[0], points, points)
    )
    return lax.linalg.tridiagonal_solve(lower, main, upper, ident)


def triplet_index(start, points, length):
    place = jnp.arange(points)
    rel = place[None, :] - start[:, None]
    third = length // 3
    source = jnp.where(
        rel < third,
        3 * rel,
        jnp.where(rel < 2 * third, 3 * (2 * third - 1 - rel) + 1, 3 * (rel - 2 * third) + 2),
    )
    inside = (rel >= 0) & (rel < length)
    return jnp.where(inside, source + start[:, None], place[None, :])


def triplet_apply(state, start, points):
    index = triplet_index(start, points, TRIP)
    select = (index[:, :, None] == jnp.arange(points)[None, None, :]).astype(jnp.float32)
    return jnp.einsum("lsp,lqp->lsq", state, select, precision=lax.Precision.HIGHEST)


def substep(state, active, rates, frozen_inverse):
    source = jnp.einsum("st,ltp->lsp", rates, jnp.tanh(state), precision=lax.Precision.HIGHEST)
    change = jnp.einsum("st,ltp->lsp", frozen_inverse, source, precision=lax.Precision.HIGHEST)
    return jnp.where(active[:, None, None], state + change, state)


def splice(state, owner, line_to, seg_from, seg_to, groups, slots):
    count_lines, species, points = state.shape
    segments = points // SEG
    four = state.reshape(count_lines, species, segments, SEG)
    seg_place = jnp.arange(segments)
    picking = (seg_from[:, None] == seg_place[None, :]).astype(jnp.float32)
    outgoing = jnp.einsum("lsnk,ln->lsk", four, picking, precision=lax.Precision.HIGHEST).reshape(
        count_lines, species * SEG
    )
    order = jnp.arange(count_lines)
    earlier = (owner[:, None] == owner[None, :]) & (order[:, None] > order[None, :])
    ranks = jnp.sum(earlier.astype(jnp.int32), axis=1)
    position = owner * slots + ranks
    placing = (jnp.arange(groups * slots)[:, None] == position[None, :]).astype(jnp.float32)
    sending = jnp.dot(placing, outgoing, precision=lax.Precision.HIGHEST)
    code_plus = (line_to * segments + seg_to + 1).astype(jnp.float32)
    aiming = jnp.dot(placing, code_plus, precision=lax.Precision.HIGHEST) - 1.0
    received, aims = (
        lax.all_to_all(
            sending.reshape(groups, slots, species * SEG),
            ("grid", "line"),
            split_axis=0,
            concat_axis=0,
            tiled=True,
        ),
        lax.all_to_all(
            aiming.reshape(groups, slots), ("grid", "line"), split_axis=0, concat_axis=0, tiled=True
        ),
    )
    received = received.reshape(groups * slots, species * SEG)
    aims = aims.reshape(groups * slots)
    live = aims >= 0.0
    landing_code = jnp.where(live, aims + 0.5, 0.0).astype(jnp.int32)
    hitting = (
        (landing_code[:, None] == jnp.arange(count_lines * segments)[None, :]) & live[:, None]
    ).astype(jnp.float32)
    gained = jnp.einsum("rc,rm->cm", hitting, received, precision=lax.Precision.HIGHEST)
    arrivals = jnp.sum(hitting, axis=0)
    gained = gained.reshape(count_lines, segments, species, SEG).transpose(0, 2, 1, 3)
    arrivals = arrivals.reshape(count_lines, 1, segments, 1)
    four = four + splice_weight * (gained - arrivals * four)
    return four.reshape(count_lines, species, points)


def body(
    les,
    lines,
    triplet_start,
    splice_owner,
    splice_line,
    splice_from,
    splice_to,
    chem_counts,
    diffusivity,
    rates,
    frozen_inverse,
):
    groups = lax.axis_size("grid") * lax.axis_size("line")
    count_lines = lines.shape[2]
    species = lines.shape[3]
    points = lines.shape[4]
    slots = max(2, 2 * count_lines // groups)
    inverse = diffusion_inverse(diffusivity, points)
    field = les
    state = lines.reshape(count_lines, species, points)
    counts = chem_counts.reshape(count_lines)
    for step in range(STEPS):
        padded = padded_2(field, (("grid", 1), ("line", 2)), 1)
        beside = (
            padded[:, 2:, 1:-1] + padded[:, :-2, 1:-1] + padded[:, 1:-1, 2:] + padded[:, 1:-1, :-2]
        )
        mid = field + les_rate * (beside - 4.0 * field)
        cellwise = mid.reshape(species, count_lines).T
        state = state + relax_rate * (cellwise - jnp.mean(state, axis=2))[:, :, None]
        state = triplet_apply(state, triplet_start[step].reshape(count_lines), points)
        state = jnp.einsum("lsp,sqp->lsq", state, inverse, precision=lax.Precision.HIGHEST)
        turns = jnp.max(counts)

        def advance(sub, current):
            return substep(current, counts > sub, rates, frozen_inverse)

        state = lax.fori_loop(0, turns, advance, state)
        state = splice(
            state,
            splice_owner[step].reshape(count_lines),
            splice_line[step].reshape(count_lines),
            splice_from[step].reshape(count_lines),
            splice_to[step].reshape(count_lines),
            groups,
            slots,
        )
        filtered = jnp.mean(state, axis=2)
        field = 0.5 * mid + 0.5 * filtered.T.reshape(field.shape)
    return (field, state.reshape(lines.shape))


def solution(mesh):
    in_specs = (
        P(None, "grid", "line"),
        P("grid", "line", None, None, None),
        P(None, "grid", "line", None),
        P(None, "grid", "line", None, None),
        P(None, "grid", "line", None),
        P(None, "grid", "line", None),
        P(None, "grid", "line", None),
        P("grid", "line", None),
        P(),
        P(),
        P(),
    )
    out_specs = (P(None, "grid", "line"), P("grid", "line", None, None, None))
    return jax.shard_map(body, mesh=mesh, in_specs=in_specs, out_specs=out_specs, check_vma=False)
```

profile of v0, /device:TPU:0, one launch (start us, length us, event | category | flops | bytes accessed | tf_op | source)
XLA Modules:
  0.0 240.2 jit_solution(3991907475050814731)
XLA Ops:
  1.4 5.0 %collective-permute-start.1 = (f32[24,1,128]{0,2,1:T(8,128)S(1)}, f32[24,1,128]{0,2,1:T(8,128)S(1)}, u32[]{:S(2)}, u32[]{:S(2)}) collective-permute-start(f32[24,1,128]{0,2,1:T(8,128)S(1)} %copy.398), channel_id=1, source_target_pairs={{0,8},{8,16},{16,24},{1,9},{9,17},{17,25},{2,10},{10,18},{18,26},{... | collective-permute-start | bytes 36872 | tf_op jit(solution)/shard_map/ppermute | solution.py:23
  11.4 7.0 %all-to-all-start = ((f32[32,1,8]{2,1,0:T(1,128)}), f32[32,1,8]{2,1,0:T(1,128)}, u32[]{:S(2)}, u32[]{:S(2)}) async-start(f32[32,1,8]{2,1,0:T(1,128)} %bitcast.607), calls=%async_computation | async-start | bytes 32768 | tf_op jit(solution)/shard_map/all_to_all | solution.py:93
  22.9 10.4 %while.52 = (s32[]{:T(128)}, f32[24]{0:T(128)S(1)}, f32[24,128]{1,0:T(8,128)S(1)}, f32[3,32,24]{2,1,0:T(8,128)S(1)}, f32[3,32,24,128]{3,2,1,0:T(8,128)S(1)}, /*i...) while((s32[]{:T(128)}, f32[24]{0:T(128)S(1)}, ...), condition=%wide.region_1.2_spmd, body=%wide.region_0.1_spmd.sunk | while | flops 445425 | bytes 2483921 | solution.py:40
  53.2 7.2 %while.53 = (s32[]{:T(128)}, f32[24,128]{1,0:T(8,128)S(1)}, f32[3,32,24,128]{3,1,0,2:T(8,128)}, f32[3,32,24,128]{3,2,1,0:T(8,128)S(1)}, f32[3,32,24]{2,1,0:T(8,1...) while((s32[]{:T(128)}, f32[24,128]{1,0:T(8,128)S(1)}, ...), condition=%wide.region_3.4_spmd, body=%wide.region_2.3_spmd.sunk | while | flops 288801 | bytes 2389165 | solution.py:40
  62.9 2.0 fusion.467
  68.8 3.6 %collective-permute-start.3 = (f32[24,3,1]{2,0,1:T(8,128)}, f32[24,3,1]{2,0,1:T(8,128)}, u32[]{:S(2)}, u32[]{:S(2)}) collective-permute-start(f32[24,3,1]{2,0,1:T(8,128)} %get-tuple-element.764), channel_id=1, source_target_pairs={{0,1},{1,2},{2,3},{3,4},{4,5},{5,6},{6,7},{8,9},{9,10},{10,11},{11... | collective-permute-start | bytes 872 | tf_op jit(solution)/shard_map/ppermute | solution.py:23
  72.4 7.1 %concatenate.52 = f32[127,24,128]{2,0,1:T(8,128)S(1)} concatenate(f32[1,24,128]{2,0,1:T(1,128)S(1)} %bitcast.2693, f32[1,24,128]{2,0,1:T(1,128)S(1)} %bitcast.2694, f32[1,24,128]{2,0,1:T(1,128)} %bitcast.2695, f32[1,24,128]{2,0,1:T(1,128)} %bitcast.2696, f32[1,24,128]{2,0,1:T(1,128)} %bitcast.2697, f32[1,24,128]{2,0,1:T(1,128)} %bitcast.2698, f32[1,24,128]{2,0,1:T(1,128)} %bitcast.2699, ...), dimensions={0} | concatenate | bytes 3121152 | tf_op jit(solution)/shard_map/vmap()/concatenate | solution.py:40
  84.0 10.0 %fusion.368 = f32[128,24,128]{2,1,0:T(8,128)S(1)} fusion(s32[128,128]{1,0:T(8,128)S(1)} %iota_select_fusion.1, f32[1,1,128,24,128]{4,3,2,1,0:T(8,128)S(1)} %copy-done.2, f32[128,24]{1,0:T(8,128)S(1)} %get-tuple-element.644), kind=kOutput, calls=%fused_computation.629 | convolution fusion | flops 606470144 | bytes 3223552 | tf_op jit(solution)/shard_map/lsp,lqp->lsq/dot_general | solution.py:59
  94.0 3.4 %fusion.381 = f32[128,24,128]{0,2,1:T(8,128)S(1)} fusion(f32[128,24,128]{2,1,0:T(8,128)S(1)} %fusion.368, f32[24,127,128]{2,1,0:T(8,128)S(1)} %bitcast.2635, f32[24,1,128]{2,1,0:T(1,128)S(1)} %bitcast.2673), kind=kOutput, calls=%fused_computation.648 | convolution fusion | flops 604372992 | bytes 4718592 | tf_op jit(solution)/shard_map/lsp,sqp->lsq/dot_general | solution.py:143
  98.2 27.3 %while.54 = (s32[]{:T(128)}, f32[128,24,128]{2,1,0:T(8,128)S(1)}, s32[]{:T(128)}, s32[128]{0:T(128)S(1)}, f32[24,24]{1,0:T(8,128)S(1)}, /*index=5*/f32[24,24]{1,0:T(8,128)S(1)}, s32[]{:T(128)}) while((s32[]{:T(128)}, f32[128,24,128]{2,1,0:T(8,128)S(1)}, s32[]{:T(128)}, s32[128]{0:T(128)S(1)}, f32[24,24]{1,0:T(8,128)S(1)}, ...), condition=%wide.region_7.8_spmd, body=%wide.region_6.7_spmd.sunk | while | flops 227278976 | bytes 7869777 | solution.py:149
  98.9 1.6 fusion.802
  100.4 2.2 add_select_fusion.4
  103.3 1.6 fusion.802
  104.9 2.2 add_select_fusion.4
  107.7 1.6 fusion.802
  109.3 2.2 add_select_fusion.4
  112.2 1.6 fusion.802
  113.8 2.2 add_select_fusion.4
  116.6 1.6 fusion.802
  118.2 2.2 add_select_fusion.4
  121.1 1.6 fusion.802
  122.7 2.2 add_select_fusion.4
  128.0 6.3 %all-to-all-start.1 = ((f32[32,8,384]{2,1,0:T(8,128)}), f32[32,8,384]{2,1,0:T(8,128)S(1)}, u32[]{:S(2)}, u32[]{:S(2)}) async-start(f32[32,8,384]{2,1,0:T(8,128)} %fusion.409), calls=%async_computation.1 | async-start | bytes 786432 | tf_op jit(solution)/shard_map/all_to_all | solution.py:86
  138.4 9.2 %all-to-all-done.1 = f32[32,8,384]{2,1,0:T(8,128)S(1)} async-done(((f32[32,8,384]{2,1,0:T(8,128)}), f32[32,8,384]{2,1,0:T(8,128)S(1)}, u32[]{:S(2)}, u32[]{:S(2)}) %all-to-all-start.1) | async-done | bytes 393248 | tf_op jit(solution)/shard_map/all_to_all | solution.py:86
  147.6 3.1 %all-to-all-start.2 = ((f32[32,1,8]{2,1,0:T(1,128)}), f32[32,1,8]{2,1,0:T(1,128)}, u32[]{:S(2)}, u32[]{:S(2)}) async-start(f32[32,1,8]{2,1,0:T(1,128)} %bitcast.632), calls=%async_computation.2 | async-start | bytes 32768 | tf_op jit(solution)/shard_map/all_to_all | solution.py:93
  150.8 2.6 %fusion.742 = (f32[128,24]{0,1:T(8,128)}, f32[128,24,8,16]{0,1,3,2:T(8,128)S(1)}) fusion(f32[128,24,8,16]{0,1,3,2:T(8,128)S(1)} %bitcast.2632, f32[128,8]{0,1:T(8,128)} %copy.470, f32[24,16,256]{2,1,0:T(8,128)S(1)} %bitcast.2648, s32[128,8]{0,1:T(8,128)S(1)} %multiply_add_fusion.4, s32[256]{0:T(256)} %copy-done.49, pred[256]{0:T(512)(128)(4,1)} %copy-done.58), kind=kOutput, calls=%fused_computation.1135 | convolution fusion | flops 1210446848 | bytes 3560704 | tf_op jit(solution)/shard_map/rc,rm->cm/dot_general | solution.py:104
  155.1 3.5 %collective-permute-start.5 = (f32[24,1,128]{0,2,1:T(8,128)S(1)}, f32[24,1,128]{0,2,1:T(8,128)S(1)}, u32[]{:S(2)}, u32[]{:S(2)}) collective-permute-start(f32[24,1,128]{0,2,1:T(8,128)S(1)} %broadcast_multiply_fusion), channel_id=1, source_target_pairs={{0,8},{8,16},{16,24},{1,9},{9,17},{17,25},{2,10},{10,18},{18,26},{... | collective-permute-start | bytes 36872 | tf_op jit(solution)/shard_map/ppermute | solution.py:23
  161.0 3.8 %collective-permute-done.4 = f32[24,1,128]{0,2,1:T(8,128)S(1)} collective-permute-done((f32[24,1,128]{0,2,1:T(8,128)S(1)}, f32[24,1,128]{0,2,1:T(8,128)S(1)}, u32[]{:S(2)}, u32[]{:S(2)}) %collective-permute-start.4) | collective-permute-done | bytes 12320 | tf_op jit(solution)/shard_map/ppermute | solution.py:24
  166.8 3.6 %collective-permute-start.7 = (f32[24,3,1]{2,0,1:T(8,128)}, f32[24,3,1]{2,0,1:T(8,128)}, u32[]{:S(2)}, u32[]{:S(2)}) collective-permute-start(f32[24,3,1]{2,0,1:T(8,128)} %get-tuple-element.760), channel_id=1, source_target_pairs={{0,1},{1,2},{2,3},{3,4},{4,5},{5,6},{6,7},{8,9},{9,10},{10,11},{11... | collective-permute-start | bytes 872 | tf_op jit(solution)/shard_map/ppermute | solution.py:23
  174.3 10.0 %fusion.369 = f32[128,24,128]{2,1,0:T(8,128)S(1)} fusion(s32[128,128]{1,0:T(8,128)S(1)} %iota_select_fusion, f32[128,24,128]{2,1,0:T(8,128)S(1)} %copy.477, f32[128,24]{1,0:T(8,128)S(1)} %get-tuple-element.544), kind=kOutput, calls=%fused_computation.630 | convolution fusion | flops 606470144 | bytes 3223552 | tf_op jit(solution)/shard_map/lsp,lqp->lsq/dot_general | solution.py:59
  184.4 3.4 %fusion.384 = f32[128,24,128]{0,2,1:T(8,128)S(1)} fusion(f32[128,24,128]{2,1,0:T(8,128)S(1)} %fusion.369, f32[24,127,128]{2,1,0:T(8,128)S(1)} %bitcast.2636, f32[24,1,128]{2,1,0:T(1,128)S(1)} %bitcast.2674), kind=kOutput, calls=%fused_computation.649 | convolution fusion | flops 604372992 | bytes 4718592 | tf_op jit(solution)/shard_map/lsp,sqp->lsq/dot_general | solution.py:143
  188.5 27.3 %while.55 = (s32[]{:T(128)}, f32[128,24,128]{2,1,0:T(8,128)S(1)}, s32[]{:T(128)}, s32[128]{0:T(128)S(1)}, f32[24,24]{1,0:T(8,128)S(1)}, /*index=5*/f32[24,24]{1,0:T(8,128)S(1)}, s32[]{:T(128)}) while((s32[]{:T(128)}, f32[128,24,128]{2,1,0:T(8,128)S(1)}, s32[]{:T(128)}, s32[128]{0:T(128)S(1)}, f32[24,24]{1,0:T(8,128)S(1)}, ...), condition=%wide.region_12.13_spmd, body=%wide.region_11.12_spmd.sunk | while | flops 227278976 | bytes 7869777 | solution.py:149
  189.2 1.6 fusion.807
  190.7 2.2 add_select_fusion.5
  193.6 1.6 fusion.807
  195.2 2.2 add_select_fusion.5
  198.1 1.6 fusion.807
  199.6 2.2 add_select_fusion.5
  202.5 1.6 fusion.807
  204.1 2.2 add_select_fusion.5
  206.9 1.6 fusion.807
  208.5 2.2 add_select_fusion.5
  211.4 1.6 fusion.807
  213.0 2.2 add_select_fusion.5
  218.3 4.2 %all-to-all-start.3 = ((f32[32,8,384]{2,1,0:T(8,128)}), f32[32,8,384]{2,1,0:T(8,128)S(1)}, u32[]{:S(2)}, u32[]{:S(2)}) async-start(f32[32,8,384]{2,1,0:T(8,128)} %fusion.407), calls=%async_computation.3 | async-start | bytes 786432 | tf_op jit(solution)/shard_map/all_to_all | solution.py:86
  225.8 9.6 %all-to-all-done.3 = f32[32,8,384]{2,1,0:T(8,128)S(1)} async-done(((f32[32,8,384]{2,1,0:T(8,128)}), f32[32,8,384]{2,1,0:T(8,128)S(1)}, u32[]{:S(2)}, u32[]{:S(2)}) %all-to-all-start.3) | async-done | bytes 393248 | tf_op jit(solution)/shard_map/all_to_all | solution.py:86
  235.7 2.0 fusion.743
  237.7 1.7 copy.488
  (682 shorter events, 81.1 us)
Async XLA Ops:
  1.4 65.2 %collective-permute-start.1 = (f32[24,1,128]{0,2,1:T(8,128)S(1)}, f32[24,1,128]{0,2,1:T(8,128)S(1)}, u32[]{:S(2)}, u32[]{:S(2)}) collective-permute-start(f32[24,1,128]{0,2,1:T(8,128)S(1)} %copy.398), channel_id=1, source_target_pairs={{0,8},{8,16},{16,24},{1,9},{9,17},{17,25},{2,10},{10,18},{18,26},{... | collective-permute-start | bytes 36872 | tf_op jit(solution)/shard_map/ppermute | solution.py:23
  6.4 60.3 %collective-permute-start = (f32[24,1,128]{0,2,1:T(8,128)S(1)}, f32[24,1,128]{0,2,1:T(8,128)S(1)}, u32[]{:S(2)}, u32[]{:S(2)}) collective-permute-start(f32[24,1,128]{0,2,1:T(8,128)S(1)} %copy.398), channel_id=1, source_target_pairs={{8,0},{16,8},{24,16},{9,1},{17,9},{25,17},{10,2},{18,10},{26,18},{... | collective-permute-start | bytes 36872 | tf_op jit(solution)/shard_map/ppermute | solution.py:24
  11.4 116.6 %all-to-all-start = ((f32[32,1,8]{2,1,0:T(1,128)}), f32[32,1,8]{2,1,0:T(1,128)}, u32[]{:S(2)}, u32[]{:S(2)}) async-start(f32[32,1,8]{2,1,0:T(1,128)} %bitcast.607), calls=%async_computation | async-start | bytes 32768 | tf_op jit(solution)/shard_map/all_to_all | solution.py:93
  39.4 9.9 %copy-start.21 = (f32[24]{0:T(128)S(1)}, f32[24]{0:T(128)}, u32[]{:S(2)}) copy-start(f32[24]{0:T(128)} %get-tuple-element.752) | copy-start | bytes 292
  39.4 9.9 %copy-start.22 = (f32[128]{0:T(128)S(1)}, f32[128]{0:T(128)}, u32[]{:S(2)}) copy-start(f32[128]{0:T(128)} %get-tuple-element.739) | copy-start | bytes 1540
  39.5 10.0 %copy-start.23 = (f32[24]{0:T(128)S(1)}, f32[24]{0:T(128)}, u32[]{:S(2)}) copy-start(f32[24]{0:T(128)} %get-tuple-element.753) | copy-start | bytes 292
  39.5 10.0 %copy-start.29 = (f32[128]{0:T(128)S(1)}, f32[128]{0:T(128)}, u32[]{:S(2)}) copy-start(f32[128]{0:T(128)} %get-tuple-element.740) | copy-start | bytes 1540
  39.5 10.1 %copy-start.31 = (f32[24]{0:T(128)S(1)}, f32[24]{0:T(128)}, u32[]{:S(2)}) copy-start(f32[24]{0:T(128)} %get-tuple-element.745) | copy-start | bytes 292
  39.5 10.1 %copy-start.37 = (f32[128]{0:T(128)S(1)}, f32[128]{0:T(128)}, u32[]{:S(2)}) copy-start(f32[128]{0:T(128)} %get-tuple-element.732) | copy-start | bytes 1540
  39.5 10.2 %copy-start.41 = (f32[24]{0:T(128)S(1)}, f32[24]{0:T(128)}, u32[]{:S(2)}) copy-start(f32[24]{0:T(128)} %get-tuple-element.713) | copy-start | bytes 292
  39.5 10.2 %copy-start.42 = (f32[128]{0:T(128)S(1)}, f32[128]{0:T(128)}, u32[]{:S(2)}) copy-start(f32[128]{0:T(128)} %get-tuple-element.694) | copy-start | bytes 1540
  39.5 10.3 %copy-start.51 = (f32[24]{0:T(128)S(1)}, f32[24]{0:T(128)}, u32[]{:S(2)}) copy-start(f32[24]{0:T(128)} %get-tuple-element.587) | copy-start | bytes 292
  39.5 10.3 %copy-start.55 = (f32[24]{0:T(128)S(1)}, f32[24]{0:T(128)}, u32[]{:S(2)}) copy-start(f32[24]{0:T(128)} %get-tuple-element.754) | copy-start | bytes 292
  52.9 9.7 %copy-start.66 = (f32[24]{0:T(128)S(1)}, f32[24]{0:T(128)}, u32[]{:S(2)}) copy-start(f32[24]{0:T(128)} %get-tuple-element.334) | copy-start | bytes 292
  52.9 9.7 %copy-start.67 = (f32[24]{0:T(128)S(1)}, f32[24]{0:T(128)}, u32[]{:S(2)}) copy-start(f32[24]{0:T(128)} %get-tuple-element.335) | copy-start | bytes 292
  52.9 9.6 %copy-start.68 = (f32[24]{0:T(128)S(1)}, f32[24]{0:T(128)}, u32[]{:S(2)}) copy-start(f32[24]{0:T(128)} %get-tuple-element.336) | copy-start | bytes 292
  52.9 9.6 %copy-start.69 = (f32[24]{0:T(128)S(1)}, f32[24]{0:T(128)}, u32[]{:S(2)}) copy-start(f32[24]{0:T(128)} %get-tuple-element.337) | copy-start | bytes 292
  53.0 9.6 %copy-start.70 = (f32[24]{0:T(128)S(1)}, f32[24]{0:T(128)}, u32[]{:S(2)}) copy-start(f32[24]{0:T(128)} %get-tuple-element.338) | copy-start | bytes 292
  53.0 9.6 %copy-start.71 = (f32[24]{0:T(128)S(1)}, f32[24]{0:T(128)}, u32[]{:S(2)}) copy-start(f32[24]{0:T(128)} %get-tuple-element.339) | copy-start | bytes 292
  53.0 9.6 %copy-start.72 = (f32[24]{0:T(128)S(1)}, f32[24]{0:T(128)}, u32[]{:S(2)}) copy-start(f32[24]{0:T(128)} %get-tuple-element.340) | copy-start | bytes 292
  53.0 9.6 %copy-start.73 = (f32[24]{0:T(128)S(1)}, f32[24]{0:T(128)}, u32[]{:S(2)}) copy-start(f32[24]{0:T(128)} %get-tuple-element.341) | copy-start | bytes 292
  53.0 9.6 %copy-start.74 = (f32[24]{0:T(128)S(1)}, f32[24]{0:T(128)}, u32[]{:S(2)}) copy-start(f32[24]{0:T(128)} %get-tuple-element.342) | copy-start | bytes 292
  53.0 9.6 %copy-start.75 = (f32[24]{0:T(128)S(1)}, f32[24]{0:T(128)}, u32[]{:S(2)}) copy-start(f32[24]{0:T(128)} %get-tuple-element.343) | copy-start | bytes 292
  53.0 9.6 %copy-start.76 = (f32[24]{0:T(128)S(1)}, f32[24]{0:T(128)}, u32[]{:S(2)}) copy-start(f32[24]{0:T(128)} %get-tuple-element.344) | copy-start | bytes 292
  53.0 9.6 %copy-start.77 = (f32[24]{0:T(128)S(1)}, f32[24]{0:T(128)}, u32[]{:S(2)}) copy-start(f32[24]{0:T(128)} %get-tuple-element.345) | copy-start | bytes 292
  53.0 9.6 %copy-start.78 = (f32[24]{0:T(128)S(1)}, f32[24]{0:T(128)}, u32[]{:S(2)}) copy-start(f32[24]{0:T(128)} %get-tuple-element.346) | copy-start | bytes 292
  53.0 9.6 %copy-start.79 = (f32[24]{0:T(128)S(1)}, f32[24]{0:T(128)}, u32[]{:S(2)}) copy-start(f32[24]{0:T(128)} %get-tuple-element.347) | copy-start | bytes 292
  53.1 9.6 %copy-start.80 = (f32[24]{0:T(128)S(1)}, f32[24]{0:T(128)}, u32[]{:S(2)}) copy-start(f32[24]{0:T(128)} %get-tuple-element.348) | copy-start | bytes 292
  53.1 9.6 %copy-start.81 = (f32[24]{0:T(128)S(1)}, f32[24]{0:T(128)}, u32[]{:S(2)}) copy-start(f32[24]{0:T(128)} %get-tuple-element.349) | copy-start | bytes 292
  53.1 9.6 %copy-start.82 = (f32[24]{0:T(128)S(1)}, f32[24]{0:T(128)}, u32[]{:S(2)}) copy-start(f32[24]{0:T(128)} %get-tuple-element.350) | copy-start | bytes 292
  53.1 9.6 %copy-start.83 = (f32[24]{0:T(128)S(1)}, f32[24]{0:T(128)}, u32[]{:S(2)}) copy-start(f32[24]{0:T(128)} %get-tuple-element.351) | copy-start | bytes 292
  53.1 9.6 %copy-start.84 = (f32[24]{0:T(128)S(1)}, f32[24]{0:T(128)}, u32[]{:S(2)}) copy-start(f32[24]{0:T(128)} %get-tuple-element.352) | copy-start | bytes 292
  53.1 9.6 %copy-start.85 = (f32[24]{0:T(128)S(1)}, f32[24]{0:T(128)}, u32[]{:S(2)}) copy-start(f32[24]{0:T(128)} %get-tuple-element.353) | copy-start | bytes 292
  53.1 9.6 %copy-start.86 = (f32[24]{0:T(128)S(1)}, f32[24]{0:T(128)}, u32[]{:S(2)}) copy-start(f32[24]{0:T(128)} %get-tuple-element.354) | copy-start | bytes 292
  53.2 12.2 %copy-start.2 = (f32[1,1,128,24,128]{4,3,2,1,0:T(8,128)S(1)}, f32[1,1,128,24,128]{4,3,2,1,0:T(8,128)}, u32[]{:S(2)}) copy-start(f32[1,1,128,24,128]{4,3,2,1,0:T(8,128)} %param.20) | copy-start | bytes 4718596
  67.5 12.0 %collective-permute-start.2 = (f32[24,3,1]{2,0,1:T(8,128)}, f32[24,3,1]{2,0,1:T(8,128)}, u32[]{:S(2)}, u32[]{:S(2)}) collective-permute-start(f32[24,3,1]{2,0,1:T(8,128)} %get-tuple-element.763), channel_id=1, source_target_pairs={{1,0},{2,1},{3,2},{4,3},{5,4},{6,5},{7,6},{9,8},{10,9},{11,10},{12... | collective-permute-start | bytes 872 | tf_op jit(solution)/shard_map/ppermute | solution.py:24
  68.8 10.7 %collective-permute-start.3 = (f32[24,3,1]{2,0,1:T(8,128)}, f32[24,3,1]{2,0,1:T(8,128)}, u32[]{:S(2)}, u32[]{:S(2)}) collective-permute-start(f32[24,3,1]{2,0,1:T(8,128)} %get-tuple-element.764), channel_id=1, source_target_pairs={{0,1},{1,2},{2,3},{3,4},{4,5},{5,6},{6,7},{8,9},{9,10},{10,11},{11... | collective-permute-start | bytes 872 | tf_op jit(solution)/shard_map/ppermute | solution.py:23
  79.5 14.5 %copy-start = (f32[127,24,128]{2,0,1:T(8,128)}, f32[127,24,128]{2,0,1:T(8,128)S(1)}, u32[]{:S(2)}) copy-start(f32[127,24,128]{2,0,1:T(8,128)S(1)} %concatenate.52) | copy-start | bytes 4681732
  84.0 10.0 %copy-start.12 = (f32[24,128]{1,0:T(8,128)S(1)}, f32[24,128]{1,0:T(8,128)}, u32[]{:S(2)}) copy-start(f32[24,128]{1,0:T(8,128)} %get-tuple-element.546) | copy-start | bytes 36868
  128.0 19.5 %all-to-all-start.1 = ((f32[32,8,384]{2,1,0:T(8,128)}), f32[32,8,384]{2,1,0:T(8,128)S(1)}, u32[]{:S(2)}, u32[]{:S(2)}) async-start(f32[32,8,384]{2,1,0:T(8,128)} %fusion.409), calls=%async_computation.1 | async-start | bytes 786432 | tf_op jit(solution)/shard_map/all_to_all | solution.py:86
  147.6 70.8 %all-to-all-start.2 = ((f32[32,1,8]{2,1,0:T(1,128)}), f32[32,1,8]{2,1,0:T(1,128)}, u32[]{:S(2)}, u32[]{:S(2)}) async-start(f32[32,1,8]{2,1,0:T(1,128)} %bitcast.632), calls=%async_computation.2 | async-start | bytes 32768 | tf_op jit(solution)/shard_map/all_to_all | solution.py:93
  155.1 5.8 %collective-permute-start.5 = (f32[24,1,128]{0,2,1:T(8,128)S(1)}, f32[24,1,128]{0,2,1:T(8,128)S(1)}, u32[]{:S(2)}, u32[]{:S(2)}) collective-permute-start(f32[24,1,128]{0,2,1:T(8,128)S(1)} %broadcast_multiply_fusion), channel_id=1, source_target_pairs={{0,8},{8,16},{16,24},{1,9},{9,17},{17,25},{2,10},{10,18},{18,26},{... | collective-permute-start | bytes 36872 | tf_op jit(solution)/shard_map/ppermute | solution.py:23
  158.6 6.2 %collective-permute-start.4 = (f32[24,1,128]{0,2,1:T(8,128)S(1)}, f32[24,1,128]{0,2,1:T(8,128)S(1)}, u32[]{:S(2)}, u32[]{:S(2)}) collective-permute-start(f32[24,1,128]{0,2,1:T(8,128)S(1)} %broadcast_multiply_fusion), channel_id=1, source_target_pairs={{8,0},{16,8},{24,16},{9,1},{17,9},{25,17},{10,2},{18,10},{26,18},{... | collective-permute-start | bytes 36872 | tf_op jit(solution)/shard_map/ppermute | solution.py:24
  165.5 7.1 %collective-permute-start.6 = (f32[24,3,1]{2,0,1:T(8,128)}, f32[24,3,1]{2,0,1:T(8,128)}, u32[]{:S(2)}, u32[]{:S(2)}) collective-permute-start(f32[24,3,1]{2,0,1:T(8,128)} %get-tuple-element.759), channel_id=1, source_target_pairs={{1,0},{2,1},{3,2},{4,3},{5,4},{6,5},{7,6},{9,8},{10,9},{11,10},{12... | collective-permute-start | bytes 872 | tf_op jit(solution)/shard_map/ppermute | solution.py:24
  166.8 5.8 %collective-permute-start.7 = (f32[24,3,1]{2,0,1:T(8,128)}, f32[24,3,1]{2,0,1:T(8,128)}, u32[]{:S(2)}, u32[]{:S(2)}) collective-permute-start(f32[24,3,1]{2,0,1:T(8,128)} %get-tuple-element.760), channel_id=1, source_target_pairs={{0,1},{1,2},{2,3},{3,4},{4,5},{5,6},{6,7},{8,9},{9,10},{10,11},{11... | collective-permute-start | bytes 872 | tf_op jit(solution)/shard_map/ppermute | solution.py:23
  174.3 10.0 %copy-start.1 = (f32[127,24,128]{2,0,1:T(8,128)S(1)}, f32[127,24,128]{2,0,1:T(8,128)}, u32[]{:S(2)}) copy-start(f32[127,24,128]{2,0,1:T(8,128)} %copy-done) | copy-start | bytes 4681732
  174.3 10.0 %copy-start.13 = (f32[24,128]{1,0:T(8,128)S(1)}, f32[24,128]{1,0:T(8,128)}, u32[]{:S(2)}) copy-start(f32[24,128]{1,0:T(8,128)} %get-tuple-element.546) | copy-start | bytes 36868
  218.3 17.2 %all-to-all-start.3 = ((f32[32,8,384]{2,1,0:T(8,128)}), f32[32,8,384]{2,1,0:T(8,128)S(1)}, u32[]{:S(2)}, u32[]{:S(2)}) async-start(f32[32,8,384]{2,1,0:T(8,128)} %fusion.407), calls=%async_computation.3 | async-start | bytes 786432 | tf_op jit(solution)/shard_map/all_to_all | solution.py:86
  (73 other events, 373.5 us)
where the time goes:
time: 243 us; the launch traced here: 240 us
  matrix products  80.4 us (33%)
  other arithmetic  42.8 us (18%)
  starting transfers between devices  41.7 us (17%)
  local copies, waits for them, and re-layouts  39.8 us (16%)
  waiting for transfers between devices  22.7 us (9%)
  loops' own time  9.96 us (4%)
  between operations  2.72 us (1%)
    dot_general x12, matrix products, substep(): jnp.einsum('st,ltp->lsp', frozen_inverse, source, precision=lax.Precision...  26.6 us
    dot_general x2, matrix products, triplet_apply(): jnp.einsum('lsp,lqp->lsq', state, select, precision=lax.Precision.HIGHEST)  20 us
    all_to_all x2, waiting for transfers between devices, splice(): lax.all_to_all(sending.reshape(groups, slots, species * SEG), ('grid', 'l...  18.8 us
    dot_general x12, matrix products, substep(): jnp.einsum('st,ltp->lsp', rates, jnp.tanh(state), precision=lax.Precision...  18.6 us
    ppermute x4, starting transfers between devices, padded_2(): before = lax.ppermute(last, axis, up)  15.8 us
    while x135, other arithmetic  11.4 us
    unnamed x32, other arithmetic  11.3 us
    all_to_all x2, starting transfers between devices, splice(): lax.all_to_all(sending.reshape(groups, slots, species * SEG), ('grid', 'l...  10.4 us
  transfers between devices with their start and end apart: 12, of which 3 were waited for; matrix products, arithmetic and copies ran while one was open for 64% of the time, Pallas kernels for 0%

commit v1 on v0

v1 whole, which is shorter than its diff:
```python
import functools

import jax
import jax.numpy as jnp
from jax import lax
from jax.experimental import pallas as pl
from jax.experimental.pallas import tpu as pltpu
from jax.sharding import PartitionSpec as P

SEG = 16
TRIP = 48
STEPS = 2

les_rate = 0.2
relax_rate = 0.5
splice_weight = 0.5

VMEM = pl.BlockSpec(memory_space=pltpu.VMEM)
SMEM = pl.BlockSpec(memory_space=pltpu.SMEM)


def shift_along(array, axis, dim):
    peers, length = lax.axis_size(axis), array.shape[dim]
    up = [(i, i + 1) for i in range(peers - 1)]
    down = [(j, i) for i, j in up]
    before = lax.ppermute(lax.slice_in_dim(array, length - 1, length, axis=dim), axis, up)
    after = lax.ppermute(lax.slice_in_dim(array, 0, 1, axis=dim), axis, down)
    lower = jnp.concatenate([before, lax.slice_in_dim(array, 0, length - 1, axis=dim)], axis=dim)
    upper = jnp.concatenate([lax.slice_in_dim(array, 1, length, axis=dim), after], axis=dim)
    return lower + upper


def diffusion_inverse(diffusivity, points):
    coeff = diffusivity[:, None]
    root = jnp.sqrt(4.0 * coeff + 1.0)
    theta = -jnp.log(2.0 * coeff / (2.0 * coeff + 1.0 + root))
    place = jnp.arange(points, dtype=jnp.float32)
    low = 1.0 + jnp.exp(-(2.0 * place + 1.0)[None, :] * theta)
    high = 1.0 + jnp.exp(-(2.0 * (points - place) - 1.0)[None, :] * theta)
    scale = 1.0 / (root * (1.0 - jnp.exp(-2.0 * points * theta)))
    apart = jnp.abs(place[:, None] - place[None, :])
    ends = jnp.where(
        (place[:, None] <= place[None, :])[None],
        low[:, :, None] * high[:, None, :],
        low[:, None, :] * high[:, :, None],
    )
    return jnp.exp(-apart[None] * theta[:, :, None]) * ends * scale[:, :, None]


def halves(value):
    top = value.astype(jnp.bfloat16)
    return top, (value - top.astype(jnp.float32)).astype(jnp.bfloat16)


def diffuse_kernel(species, x_ref, start_ref, m_ref, o_ref):
    points = x_ref.shape[1]
    lines = x_ref.shape[0] // species
    start = start_ref[...]
    place = lax.broadcasted_iota(jnp.int32, (lines, points), 1)
    rel = place - start
    third = TRIP // 3
    source = jnp.where(
        rel < third,
        3 * rel,
        jnp.where(rel < 2 * third, 3 * (2 * third - 1 - rel) + 1, 3 * (rel - 2 * third) + 2),
    )
    index = jnp.where((rel >= 0) & (rel < TRIP), source + start, place)

    def one(s, carry):
        y = x_ref[pl.ds(s, lines, stride=species), :]
        y = jnp.take_along_axis(y, index, axis=1, mode="promise_in_bounds")
        top, rest = halves(y)
        mtop, mrest = halves(m_ref[s])
        dot = functools.partial(jnp.dot, preferred_element_type=jnp.float32)
        out = dot(top, mtop) + dot(rest, mtop) + dot(top, mrest)
        o_ref[pl.ds(s, lines, stride=species), :] = out
        return carry

    lax.fori_loop(0, species, one, 0, unroll=4)


def chem_kernel(chunk, y_ref, mid_ref, a_ref, turns_ref, counts_ref, owner_ref, rank_ref, from_ref, o_ref, send_ref):
    lines, species, points = y_ref.shape
    lane = lax.broadcasted_iota(jnp.int32, (species, points), 1)
    send_ref[...] = jnp.zeros_like(send_ref)
    mid = mid_ref[...]

    def lift(l, carry):
        add = jnp.take_along_axis(mid, jnp.full((species, points), l, jnp.int32), axis=1, mode="promise_in_bounds")
        o_ref[l] = y_ref[l] + relax_rate * add
        return carry

    lax.fori_loop(0, lines, lift, 0, unroll=8)
    matrix = a_ref[...]

    def substep(sub, carry):
        def part(c, inner):
            base = c * chunk
            for q in range(0, chunk, 4):
                columns = []
                state = []
                for h in (0, 2):
                    y = o_ref[pl.ds(base + q + h, 2)].reshape(2 * species, points)
                    state.append(y)
                    top, rest = halves(jnp.tanh(y))
                    columns.append(jnp.concatenate([top, top, rest], axis=0))
                right = jnp.concatenate(columns, axis=1)
                change = jnp.dot(matrix, right, preferred_element_type=jnp.float32)
                for h in (0, 1):
                    for k in (0, 1):
                        l = base + q + 2 * h + k
                        factor = jnp.where(counts_ref[l] > sub, jnp.float32(1.0), jnp.float32(0.0))
                        rows = slice(k * species, (k + 1) * species)
                        o_ref[l] = state[h][rows] + factor * change[rows, h * points : (h + 1) * points]
            return inner

        return lax.fori_loop(0, lines // chunk, part, carry)

    lax.fori_loop(0, turns_ref[0], substep, 0)

    def pack(l, carry):
        slot = rank_ref[l]
        owner = owner_ref[l]
        move = (SEG * (slot - from_ref[l])) & (points - 1)
        value = pltpu.roll(o_ref[l], move, 1)
        send_ref[owner] = jnp.where(lane // SEG == slot, value, send_ref[owner])
        return carry

    lax.fori_loop(0, lines, pack, 0, unroll=8)


def land_kernel(slots, y_ref, recv_ref, aim_ref, mid_ref, o_ref, les_ref):
    lines, species, points = y_ref.shape
    groups = recv_ref.shape[0]
    segments = points // SEG
    lane = lax.broadcasted_iota(jnp.int32, (species, points), 1)
    o_ref[...] = y_ref[...]

    def land(r, carry):
        got = recv_ref[r]
        for k in range(slots):
            code = aim_ref[r * slots + k]
            safe = jnp.maximum(code, 0)
            line = safe // segments
            seg = safe - line * segments
            value = pltpu.roll(got, (SEG * (seg - k)) & (points - 1), 1)
            hit = lane // SEG == jnp.where(code >= 0, seg, -1)
            o_ref[line] = o_ref[line] + jnp.where(hit, splice_weight * (value - y_ref[line]), 0.0)
        return carry

    lax.fori_loop(0, groups, land, 0)

    def filtered(l, total):
        return jnp.where(lane == l, jnp.sum(o_ref[l], axis=1, keepdims=True), total)

    total = lax.fori_loop(0, lines, filtered, jnp.zeros((species, points), jnp.float32), unroll=8)
    les_ref[...] = 0.5 * mid_ref[...] + (0.5 / points) * total


def body(
    les,
    lines,
    triplet_start,
    splice_owner,
    splice_line,
    splice_from,
    splice_to,
    chem_counts,
    diffusivity,
    rates,
    frozen_inverse,
):
    groups = lax.axis_size("grid") * lax.axis_size("line")
    _, _, count, species, points = lines.shape
    segments = points // SEG
    slots = min(segments, max(2, 2 * count // groups))
    f32 = jnp.float32
    params = pltpu.CompilerParams(vmem_limit_bytes=40 * 1024 * 1024)

    mixing = diffusion_inverse(diffusivity, points) - relax_rate / points
    joint = jnp.dot(frozen_inverse, rates, precision=lax.Precision.HIGHEST)
    twice = jnp.kron(jnp.eye(2, dtype=f32), joint)
    top = lax.reduce_precision(twice, 8, 7)
    rest = lax.reduce_precision(twice - top, 8, 7)
    matrix = jnp.concatenate([top, rest, top], axis=1).astype(jnp.bfloat16)

    starts = triplet_start.reshape(STEPS, count, 1)
    owner = splice_owner.reshape(STEPS, count)
    line_to = splice_line.reshape(STEPS, count)
    seg_from = splice_from.reshape(STEPS, count)
    seg_to = splice_to.reshape(STEPS, count)
    counts = chem_counts.reshape(count)
    turns = jnp.max(counts).reshape(1)
    order = jnp.arange(count)
    earlier = (owner[:, :, None] == owner[:, None, :]) & (order[None, :, None] > order[None, None, :])
    rank = jnp.sum(earlier.astype(jnp.int32), axis=2)
    position = owner * slots + rank
    code = (line_to * segments + seg_to).astype(f32)
    hit = jnp.arange(groups * slots)[None, :, None] == position[:, None, :]
    aims = jnp.max(jnp.where(hit, code[:, None, :], -1.0), axis=2)
    aims = aims.reshape(STEPS, groups, slots).transpose(1, 0, 2)
    aims = lax.all_to_all(aims, ("grid", "line"), split_axis=0, concat_axis=0, tiled=True)
    aims = aims.transpose(1, 0, 2).reshape(STEPS, groups * slots).astype(jnp.int32)

    diffuse = pl.pallas_call(
        functools.partial(diffuse_kernel, species),
        out_shape=jax.ShapeDtypeStruct((count * species, points), f32),
        in_specs=[VMEM] * 3,
        out_specs=VMEM,
        compiler_params=params,
        cost_estimate=pl.CostEstimate(flops=6 * species * count * points * points, bytes_accessed=5 << 20, transcendentals=0),
        name="diffuse",
    )
    block = jax.ShapeDtypeStruct((count, species, points), f32)
    chem = pl.pallas_call(
        functools.partial(chem_kernel, 32),
        out_shape=(block, jax.ShapeDtypeStruct((groups, species, points), f32)),
        in_specs=[VMEM] * 3 + [SMEM] * 5,
        out_specs=(VMEM, VMEM),
        compiler_params=params,
        name="chem",
    )
    land = pl.pallas_call(
        functools.partial(land_kernel, slots),
        out_shape=(block, jax.ShapeDtypeStruct((species, count), f32)),
        in_specs=[VMEM, VMEM, SMEM, VMEM],
        out_specs=(VMEM, VMEM),
        compiler_params=params,
        name="land",
    )

    field = les
    state = lines.reshape(count, species, points)
    for step in range(STEPS):
        beside = shift_along(field, "grid", 1) + shift_along(field, "line", 2)
        mid = (field + les_rate * (beside - 4.0 * field)).reshape(species, count)
        spread = diffuse(state.reshape(count * species, points), starts[step], mixing)
        state, sending = chem(
            spread.reshape(count, species, points), mid, matrix, turns, counts, owner[step], rank[step], seg_from[step]
        )
        received = lax.all_to_all(sending, ("grid", "line"), split_axis=0, concat_axis=0, tiled=True)
        state, field = land(state, received, aims[step], mid)
        field = field.reshape(les.shape)
    return (field, state.reshape(lines.shape))


def solution(mesh):
    in_specs = (
        P(None, "grid", "line"),
        P("grid", "line", None, None, None),
        P(None, "grid", "line", None),
        P(None, "grid", "line", None, None),
        P(None, "grid", "line", None),
        P(None, "grid", "line", None),
        P(None, "grid", "line", None),
        P("grid", "line", None),
        P(),
        P(),
        P(),
    )
    out_specs = (P(None, "grid", "line"), P("grid", "line", None, None, None))
    return jax.shard_map(body, mesh=mesh, in_specs=in_specs, out_specs=out_specs, check_vma=False)
```

time: 243 us -> 120 us (0.49)
  matrix products: 80.4 us -> 0.85 us
  Pallas kernels: 0 us -> 40.9 us
  other arithmetic: 42.8 us -> 5.33 us
  local copies, waits for them, and re-layouts: 39.8 us -> 7.91 us
  loops' own time: 9.96 us -> 0 us
  starting transfers between devices: 41.7 us -> 37 us
  waiting for transfers between devices: 22.7 us -> 26.1 us
    dot_general x34 -> x1, matrix products: 80.4 us -> 0.85 us  [body(): joint = jnp.dot(frozen_inverse, rates, precision=lax.Precision.HIGHEST)]
    pallas_call x0 -> x6, Pallas kernels: none -> 40.9 us  [the longest x2 22.7 us: body(): chem(spread.reshape(count, species, points), mid, matrix, turns, counts,...]
    while x135 -> x0, other arithmetic: 11.4 us -> none
    unnamed x32 -> x0, other arithmetic: 11.3 us -> none
    another operation x4 -> x0, loops' own time: 9.96 us -> none  [the longest x2 9.29 us: body(): state = lax.fori_loop(0, turns, advance, state)]
    concatenate x8 -> x0, local copies, waits for them, and re-layouts: 7.51 us -> none  [diffusion_inverse(): return lax.linalg.tridiagonal_solve(lower, main, upper, ident)]
    all_to_all x4 -> x3, waiting for transfers between devices: 18.8 us -> 26.1 us  [the longest x2 26.1 us: body(): lax.all_to_all(sending, ('grid', 'line'), split_axis=0, concat_axis=0, ti...]
    unnamed x229 -> x12, local copies, waits for them, and re-layouts: 9.39 us -> 2.58 us
  transfers between devices with their start and end apart: 12 -> 11, of which waited for: 3 -> 2; matrix products, arithmetic and copies ran while one was open for 64% -> 9% of each run, Pallas kernels for 0% -> 14%
where the time goes in v1:
time: 120 us; the launch traced here: 119 us
  Pallas kernels  40.9 us (34%)
  starting transfers between devices  37 us (31%)
  waiting for transfers between devices  26.1 us (22%)
  local copies, waits for them, and re-layouts  7.91 us (7%)
  other arithmetic  5.33 us (4%)
    all_to_all x2, waiting for transfers between devices, body(): lax.all_to_all(sending, ('grid', 'line'), split_axis=0, concat_axis=0, ti...  26.1 us
    pallas_call x2, Pallas kernels, body(): chem(spread.reshape(count, species, points), mid, matrix, turns, counts,...  22.7 us
    pallas_call x2, Pallas kernels, body(): state, field = land(state, received, aims[step], mid)  13 us
    all_to_all x2, starting transfers between devices, body(): lax.all_to_all(sending, ('grid', 'line'), split_axis=0, concat_axis=0, ti...  11.6 us
    ppermute x4, starting transfers between devices, shift_along(): lax.ppermute(lax.slice_in_dim(array, length - 1, length, axis=dim), axis,...  10.6 us
    all_to_all x1, starting transfers between devices, body(): lax.all_to_all(aims, ('grid', 'line'), split_axis=0, concat_axis=0, tiled...  9.7 us
    ppermute x4, starting transfers between devices, shift_along(): after = lax.ppermute(lax.slice_in_dim(array, 0, 1, axis=dim), axis, down)  5.17 us
    pallas_call x2, Pallas kernels, body(): diffuse(state.reshape(count * species, points), starts[step], mixing)  5.1 us
  transfers between devices with their start and end apart: 11, of which 2 were waited for; matrix products, arithmetic and copies ran while one was open for 9% of the time, Pallas kernels for 14%

profile of v1, /device:TPU:0, one launch (start us, length us, event | category | flops | bytes accessed | tf_op | source)
XLA Modules:
  0.0 119.0 jit_solution(4136371598850381030)
XLA Ops:
  0.6 5.0 %collective-permute-start = (f32[24,1,128]{2,0,1:T(8,128)}, f32[24,1,128]{2,0,1:T(8,128)S(1)}, u32[]{:S(2)}, u32[]{:S(2)}) collective-permute-start(f32[24,1,128]{2,0,1:T(8,128)} %bitcast.59), channel_id=1, source_target_pairs={{0,8},{8,16},{16,24},{1,9},{9,17},{17,25},{2,10},{10,18},{18,26},{... | collective-permute-start | bytes 36872 | tf_op jit(solution)/shard_map/ppermute | solution.py:26
  5.6 1.3 %collective-permute-start.1 = (f32[24,1,128]{2,0,1:T(8,128)}, f32[24,1,128]{2,0,1:T(8,128)S(1)}, u32[]{:S(2)}, u32[]{:S(2)}) collective-permute-start(f32[24,1,128]{2,0,1:T(8,128)} %bitcast.60), channel_id=1, source_target_pairs={{8,0},{16,8},{24,16},{9,1},{17,9},{25,17},{10,2},{18,10},{26,18},{... | collective-permute-start | bytes 36872 | tf_op jit(solution)/shard_map/ppermute | solution.py:27
  6.9 0.9 fusion.15
  7.8 1.4 %collective-permute-start.2 = (f32[24,1,1]{2,0,1:T(8,128)S(1)}, f32[24,1,1]{2,0,1:T(8,128)S(1)}, u32[]{:S(2)}, u32[]{:S(2)}) collective-permute-start(f32[24,1,1]{2,0,1:T(8,128)S(1)} %get-tuple-element.39), channel_id=1, source_target_pairs={{0,1},{1,2},{2,3},{3,4},{4,5},{5,6},{6,7},{8,9},{9,10},{10,11},{11... | collective-permute-start | bytes 296 | tf_op jit(solution)/shard_map/ppermute | solution.py:26
  9.2 1.3 %collective-permute-start.3 = (f32[24,1,1]{2,0,1:T(8,128)S(1)}, f32[24,1,1]{2,0,1:T(8,128)S(1)}, u32[]{:S(2)}, u32[]{:S(2)}) collective-permute-start(f32[24,1,1]{2,0,1:T(8,128)S(1)} %get-tuple-element.38), channel_id=1, source_target_pairs={{1,0},{2,1},{3,2},{4,3},{5,4},{6,5},{7,6},{9,8},{10,9},{11,10},{12... | collective-permute-start | bytes 296 | tf_op jit(solution)/shard_map/ppermute | solution.py:27
  10.5 0.9 convert_reduce_fusion
  11.5 0.7 multiply_add_fusion.1
  12.2 0.7 add_convert_fusion
  12.9 0.1 select_reduce_fusion
  13.0 0.1 reshape.387
  13.1 0.6 copy.56
  13.8 9.7 %all-to-all-start.1 = ((f32[32,2,8]{2,1,0:T(2,128)}), f32[32,2,8]{2,1,0:T(2,128)S(1)}, u32[]{:S(2)}, u32[]{:S(2)}) async-start(f32[32,2,8]{2,1,0:T(2,128)} %copy.56), calls=%async_computation.1 | async-start | bytes 65536 | tf_op jit(solution)/shard_map/all_to_all | solution.py:202
  23.5 0.9 fusion.14
  24.4 0.7 slice_bitcast_fusion.2
  25.1 0.7 multiply_divide_fusion
  25.8 0.7 slice_bitcast_fusion.3
  26.5 0.1 copy.47.start_ref
  26.6 0.8 fusion.16
  27.4 0.1 broadcast_multiply_fusion
  27.5 0.1 mul.203
  27.6 0.8 slice_bitcast_fusion
  28.4 0.1 pad_maximum_fusion.a_ref
  28.5 0.1 exponential_add_fusion.1
  28.6 1.0 multiply_add_fusion.m_ref
  29.7 2.5 %diffuse.2 = f32[3072,128]{1,0:T(8,128)S(1)} custom-call(f32[3072,128]{1,0:T(8,128)S(1)} %bitcast.51, s32[128,1]{1,0:T(8,128)S(1)} %copy.47.start_ref, f32[24,128,128]{2,1,0:T(8,128)S(1)} %multiply_add_fusion.m_ref), custom_call_target="tpu_custom_call" | custom-call | flops 301989888 | bytes 5242880 | tf_op jit(solution)/shard_map/diffuse/pallas_call | solution.py:237
  32.2 0.6 reduce_max.18
  32.9 0.1 fusion.6.mid_ref
  33.0 11.4 %chem.2 = (f32[128,24,128]{2,1,0:T(8,128)S(1)}, f32[32,24,128]{2,1,0:T(8,128)}) custom-call(f32[128,24,128]{2,1,0:T(8,128)S(1)} %bitcast.50, f32[24,128]{1,0:T(8,128)S(1)} %fusion.6.mid_ref, bf16[48,144]{1,0:T(8,128)(2,1)S(1)} %pad_maximum_fusion.a_ref, s32[1]{0:T(128)} %bitcast.12.turns_ref, s32[128]{0:T(128)S(1)} %bitcast.57, ...), custom_call_target="tpu_custom_call" | custom-call | tf_op jit(solution)/shard_map/chem/pallas_call | solution.py:238
  44.4 1.1 copy-done.1
  45.5 4.9 %all-to-all-start = ((f32[32,24,128]{2,1,0:T(8,128)}), f32[32,24,128]{2,1,0:T(8,128)S(1)}, u32[]{:S(2)}, u32[]{:S(2)}) async-start(f32[32,24,128]{2,1,0:T(8,128)} %get-tuple-element.11), calls=%async_computation | async-start | bytes 786432 | tf_op jit(solution)/shard_map/all_to_all | solution.py:241
  50.4 0.1 copy.57.start_ref
  50.5 0.1 slice_reduce_fusion
  50.6 0.1 squeeze.34.aim_ref
  50.7 12.9 %all-to-all-done.recv_ref = f32[32,24,128]{2,1,0:T(8,128)S(1)} async-done(((f32[32,24,128]{2,1,0:T(8,128)}), f32[32,24,128]{2,1,0:T(8,128)S(1)}, u32[]{:S(2)}, u32[]{:S(2)}) %all-to-all-start) | async-done | bytes 393248 | tf_op jit(solution)/shard_map/all_to_all | solution.py:241
  63.6 1.4 %copy-done.2 = f32[128,24,128]{2,1,0:T(8,128)S(1)} copy-done((f32[128,24,128]{2,1,0:T(8,128)S(1)}, f32[128,24,128]{2,1,0:T(8,128)}, u32[]{:S(2)}) %copy-start.2) | copy-done | bytes 1572888
  65.0 6.0 %land.2 = (f32[128,24,128]{2,1,0:T(8,128)S(1)}, f32[24,128]{1,0:T(8,128)S(1)}) custom-call(f32[128,24,128]{2,1,0:T(8,128)S(1)} %copy-done.2, f32[32,24,128]{2,1,0:T(8,128)S(1)} %all-to-all-done.recv_ref, s32[256]{0:T(256)S(1)} %squeeze.34.aim_ref, f32[24,128]{1,0:T(8,128)S(1)} %fusion.6.mid_ref), custom_call_target="tpu_custom_call" | custom-call | tf_op jit(solution)/shard_map/land/pallas_call | solution.py:242
  71.0 0.1 fusion.13
  71.2 2.9 %collective-permute-start.4 = (f32[24,1,128]{2,0,1:T(8,128)S(1)}, f32[24,1,128]{2,0,1:T(8,128)S(1)}, u32[]{:S(2)}, u32[]{:S(2)}) collective-permute-start(f32[24,1,128]{2,0,1:T(8,128)S(1)} %bitcast.55), channel_id=1, source_target_pairs={{0,8},{8,16},{16,24},{1,9},{9,17},{17,25},{2,10},{10,18},{18,26},{... | collective-permute-start | bytes 36872 | tf_op jit(solution)/shard_map/ppermute | solution.py:26
  74.1 1.3 %collective-permute-start.5 = (f32[24,1,128]{2,0,1:T(8,128)S(1)}, f32[24,1,128]{2,0,1:T(8,128)S(1)}, u32[]{:S(2)}, u32[]{:S(2)}) collective-permute-start(f32[24,1,128]{2,0,1:T(8,128)S(1)} %bitcast.56), channel_id=1, source_target_pairs={{8,0},{16,8},{24,16},{9,1},{17,9},{25,17},{10,2},{18,10},{26,18},{... | collective-permute-start | bytes 36872 | tf_op jit(solution)/shard_map/ppermute | solution.py:27
  75.4 1.3 %collective-permute-start.6 = (f32[24,1,1]{2,0,1:T(8,128)S(1)}, f32[24,1,1]{2,0,1:T(8,128)S(1)}, u32[]{:S(2)}, u32[]{:S(2)}) collective-permute-start(f32[24,1,1]{2,0,1:T(8,128)S(1)} %get-tuple-element.35), channel_id=1, source_target_pairs={{0,1},{1,2},{2,3},{3,4},{4,5},{5,6},{6,7},{8,9},{9,10},{10,11},{11... | collective-permute-start | bytes 296 | tf_op jit(solution)/shard_map/ppermute | solution.py:26
  76.7 1.3 %collective-permute-start.7 = (f32[24,1,1]{2,0,1:T(8,128)S(1)}, f32[24,1,1]{2,0,1:T(8,128)S(1)}, u32[]{:S(2)}, u32[]{:S(2)}) collective-permute-start(f32[24,1,1]{2,0,1:T(8,128)S(1)} %get-tuple-element.34), channel_id=1, source_target_pairs={{1,0},{2,1},{3,2},{4,3},{5,4},{6,5},{7,6},{9,8},{10,9},{11,10},{12... | collective-permute-start | bytes 296 | tf_op jit(solution)/shard_map/ppermute | solution.py:27
  78.0 2.5 %diffuse.3 = f32[3072,128]{1,0:T(8,128)S(1)} custom-call(f32[3072,128]{1,0:T(8,128)S(1)} %bitcast.52, s32[128,1]{1,0:T(8,128)S(1)} %copy.57.start_ref, f32[24,128,128]{2,1,0:T(8,128)S(1)} %multiply_add_fusion.m_ref), custom_call_target="tpu_custom_call" | custom-call | flops 301989888 | bytes 5242880 | tf_op jit(solution)/shard_map/diffuse/pallas_call | solution.py:237
  80.6 0.1 fusion.11.mid_ref
  80.6 11.4 %chem.3 = (f32[128,24,128]{2,1,0:T(8,128)S(1)}, f32[32,24,128]{2,1,0:T(8,128)}) custom-call(f32[128,24,128]{2,1,0:T(8,128)S(1)} %bitcast.49, f32[24,128]{1,0:T(8,128)S(1)} %fusion.11.mid_ref, bf16[48,144]{1,0:T(8,128)(2,1)S(1)} %pad_maximum_fusion.a_ref, s32[1]{0:T(128)} %bitcast.12.turns_ref, s32[128]{0:T(128)S(1)} %bitcast.58, ...), custom_call_target="tpu_custom_call" | custom-call | tf_op jit(solution)/shard_map/chem/pallas_call | solution.py:238
  92.0 6.7 %all-to-all-start.2 = ((f32[32,24,128]{2,1,0:T(8,128)}), f32[32,24,128]{2,1,0:T(8,128)S(1)}, u32[]{:S(2)}, u32[]{:S(2)}) async-start(f32[32,24,128]{2,1,0:T(8,128)} %get-tuple-element.15), calls=%async_computation.2 | async-start | bytes 786432 | tf_op jit(solution)/shard_map/all_to_all | solution.py:241
  98.7 0.1 squeeze.39.aim_ref
  98.8 13.2 %all-to-all-done.2.recv_ref = f32[32,24,128]{2,1,0:T(8,128)S(1)} async-done(((f32[32,24,128]{2,1,0:T(8,128)}), f32[32,24,128]{2,1,0:T(8,128)S(1)}, u32[]{:S(2)}, u32[]{:S(2)}) %all-to-all-start.2) | async-done | bytes 393248 | tf_op jit(solution)/shard_map/all_to_all | solution.py:241
  111.9 7.0 %land.3 = (f32[128,24,128]{2,1,0:T(8,128)}, f32[24,128]{1,0:T(8,128)}) custom-call(f32[128,24,128]{2,1,0:T(8,128)S(1)} %get-tuple-element.14.y_ref, f32[32,24,128]{2,1,0:T(8,128)S(1)} %all-to-all-done.2.recv_ref, s32[256]{0:T(256)S(1)} %squeeze.39.aim_ref, f32[24,128]{1,0:T(8,128)S(1)} %fusion.11.mid_ref), custom_call_target="tpu_custom_call" | custom-call | tf_op jit(solution)/shard_map/land/pallas_call | solution.py:242
  (28 shorter events, 0.2 us)
Async XLA Ops:
  0.6 26.0 %copy-start = (f32[24,24]{1,0:T(8,128)S(1)}, f32[24,24]{1,0:T(8,128)}, u32[]{:S(2)}) copy-start(f32[24,24]{1,0:T(8,128)} %param.21) | copy-start | bytes 6916
  0.6 32.2 %collective-permute-start = (f32[24,1,128]{2,0,1:T(8,128)}, f32[24,1,128]{2,0,1:T(8,128)S(1)}, u32[]{:S(2)}, u32[]{:S(2)}) collective-permute-start(f32[24,1,128]{2,0,1:T(8,128)} %bitcast.59), channel_id=1, source_target_pairs={{0,8},{8,16},{16,24},{1,9},{9,17},{17,25},{2,10},{10,18},{18,26},{... | collective-permute-start | bytes 36872 | tf_op jit(solution)/shard_map/ppermute | solution.py:26
  5.6 27.3 %collective-permute-start.1 = (f32[24,1,128]{2,0,1:T(8,128)}, f32[24,1,128]{2,0,1:T(8,128)S(1)}, u32[]{:S(2)}, u32[]{:S(2)}) collective-permute-start(f32[24,1,128]{2,0,1:T(8,128)} %bitcast.60), channel_id=1, source_target_pairs={{8,0},{16,8},{24,16},{9,1},{17,9},{25,17},{10,2},{18,10},{26,18},{... | collective-permute-start | bytes 36872 | tf_op jit(solution)/shard_map/ppermute | solution.py:27
  7.8 25.1 %collective-permute-start.2 = (f32[24,1,1]{2,0,1:T(8,128)S(1)}, f32[24,1,1]{2,0,1:T(8,128)S(1)}, u32[]{:S(2)}, u32[]{:S(2)}) collective-permute-start(f32[24,1,1]{2,0,1:T(8,128)S(1)} %get-tuple-element.39), channel_id=1, source_target_pairs={{0,1},{1,2},{2,3},{3,4},{4,5},{5,6},{6,7},{8,9},{9,10},{10,11},{11... | collective-permute-start | bytes 296 | tf_op jit(solution)/shard_map/ppermute | solution.py:26
  9.2 23.7 %collective-permute-start.3 = (f32[24,1,1]{2,0,1:T(8,128)S(1)}, f32[24,1,1]{2,0,1:T(8,128)S(1)}, u32[]{:S(2)}, u32[]{:S(2)}) collective-permute-start(f32[24,1,1]{2,0,1:T(8,128)S(1)} %get-tuple-element.38), channel_id=1, source_target_pairs={{1,0},{2,1},{3,2},{4,3},{5,4},{6,5},{7,6},{9,8},{10,9},{11,10},{12... | collective-permute-start | bytes 296 | tf_op jit(solution)/shard_map/ppermute | solution.py:27
  13.8 31.8 %all-to-all-start.1 = ((f32[32,2,8]{2,1,0:T(2,128)}), f32[32,2,8]{2,1,0:T(2,128)S(1)}, u32[]{:S(2)}, u32[]{:S(2)}) async-start(f32[32,2,8]{2,1,0:T(2,128)} %copy.56), calls=%async_computation.1 | async-start | bytes 65536 | tf_op jit(solution)/shard_map/all_to_all | solution.py:202
  27.6 2.0 %copy-start.3 = (f32[1,1,128,24,128]{4,3,2,1,0:T(8,128)S(1)}, f32[1,1,128,24,128]{4,3,2,1,0:T(8,128)}, u32[]{:S(2)}) copy-start(f32[1,1,128,24,128]{4,3,2,1,0:T(8,128)} %param.12) | copy-start | bytes 4718596
  29.6 2.6 %copy-start.4 = (s32[1,1,128]{2,1,0:T(1,128)S(1)}, s32[1,1,128]{2,1,0:T(1,128)}, u32[]{:S(2)}) copy-start(s32[1,1,128]{2,1,0:T(1,128)} %param.18) | copy-start | bytes 1540
  29.7 3.2 %copy-start.5 = (f32[24,1,128]{2,1,0:T(1,128)S(1)}, f32[24,1,128]{2,1,0:T(1,128)}, u32[]{:S(2)}) copy-start(f32[24,1,128]{2,1,0:T(1,128)} %param.11) | copy-start | bytes 36868
  44.4 1.1 copy-start.1
  45.5 18.1 %all-to-all-start = ((f32[32,24,128]{2,1,0:T(8,128)}), f32[32,24,128]{2,1,0:T(8,128)S(1)}, u32[]{:S(2)}, u32[]{:S(2)}) async-start(f32[32,24,128]{2,1,0:T(8,128)} %get-tuple-element.11), calls=%async_computation | async-start | bytes 786432 | tf_op jit(solution)/shard_map/all_to_all | solution.py:241
  63.6 1.4 %copy-start.2 = (f32[128,24,128]{2,1,0:T(8,128)S(1)}, f32[128,24,128]{2,1,0:T(8,128)}, u32[]{:S(2)}) copy-start(f32[128,24,128]{2,1,0:T(8,128)} %copy-done.1) | copy-start | bytes 4718596
  71.2 9.4 %collective-permute-start.4 = (f32[24,1,128]{2,0,1:T(8,128)S(1)}, f32[24,1,128]{2,0,1:T(8,128)S(1)}, u32[]{:S(2)}, u32[]{:S(2)}) collective-permute-start(f32[24,1,128]{2,0,1:T(8,128)S(1)} %bitcast.55), channel_id=1, source_target_pairs={{0,8},{8,16},{16,24},{1,9},{9,17},{17,25},{2,10},{10,18},{18,26},{... | collective-permute-start | bytes 36872 | tf_op jit(solution)/shard_map/ppermute | solution.py:26
  74.1 6.5 %collective-permute-start.5 = (f32[24,1,128]{2,0,1:T(8,128)S(1)}, f32[24,1,128]{2,0,1:T(8,128)S(1)}, u32[]{:S(2)}, u32[]{:S(2)}) collective-permute-start(f32[24,1,128]{2,0,1:T(8,128)S(1)} %bitcast.56), channel_id=1, source_target_pairs={{8,0},{16,8},{24,16},{9,1},{17,9},{25,17},{10,2},{18,10},{26,18},{... | collective-permute-start | bytes 36872 | tf_op jit(solution)/shard_map/ppermute | solution.py:27
  75.4 5.2 %collective-permute-start.6 = (f32[24,1,1]{2,0,1:T(8,128)S(1)}, f32[24,1,1]{2,0,1:T(8,128)S(1)}, u32[]{:S(2)}, u32[]{:S(2)}) collective-permute-start(f32[24,1,1]{2,0,1:T(8,128)S(1)} %get-tuple-element.35), channel_id=1, source_target_pairs={{0,1},{1,2},{2,3},{3,4},{4,5},{5,6},{6,7},{8,9},{9,10},{10,11},{11... | collective-permute-start | bytes 296 | tf_op jit(solution)/shard_map/ppermute | solution.py:26
  76.7 3.9 %collective-permute-start.7 = (f32[24,1,1]{2,0,1:T(8,128)S(1)}, f32[24,1,1]{2,0,1:T(8,128)S(1)}, u32[]{:S(2)}, u32[]{:S(2)}) collective-permute-start(f32[24,1,1]{2,0,1:T(8,128)S(1)} %get-tuple-element.34), channel_id=1, source_target_pairs={{1,0},{2,1},{3,2},{4,3},{5,4},{6,5},{7,6},{9,8},{10,9},{11,10},{12... | collective-permute-start | bytes 296 | tf_op jit(solution)/shard_map/ppermute | solution.py:27
  92.0 19.9 %all-to-all-start.2 = ((f32[32,24,128]{2,1,0:T(8,128)}), f32[32,24,128]{2,1,0:T(8,128)S(1)}, u32[]{:S(2)}, u32[]{:S(2)}) async-start(f32[32,24,128]{2,1,0:T(8,128)} %get-tuple-element.15), calls=%async_computation.2 | async-start | bytes 786432 | tf_op jit(solution)/shard_map/all_to_all | solution.py:241

commit v2 on v1

--- a/solution.py
+++ b/solution.py
@@ -79,7 +79,7 @@
     lax.fori_loop(0, species, one, 0, unroll=4)
 
 
-def chem_kernel(chunk, y_ref, mid_ref, a_ref, turns_ref, counts_ref, owner_ref, rank_ref, from_ref, o_ref, send_ref):
+def chem_kernel(chunk, y_ref, mid_ref, a_ref, turns_ref, counts_ref, owner_ref, rank_ref, from_ref, o_ref, send_ref, other_ref):
     lines, species, points = y_ref.shape
     lane = lax.broadcasted_iota(jnp.int32, (species, points), 1)
     send_ref[...] = jnp.zeros_like(send_ref)
@@ -93,14 +93,14 @@
     lax.fori_loop(0, lines, lift, 0, unroll=8)
     matrix = a_ref[...]
 
-    def substep(sub, carry):
+    def substep(sub, in_ref, out_ref):
         def part(c, inner):
             base = c * chunk
             for q in range(0, chunk, 4):
                 columns = []
                 state = []
                 for h in (0, 2):
-                    y = o_ref[pl.ds(base + q + h, 2)].reshape(2 * species, points)
+                    y = in_ref[pl.ds(base + q + h, 2)].reshape(2 * species, points)
                     state.append(y)
                     top, rest = halves(jnp.tanh(y))
                     columns.append(jnp.concatenate([top, top, rest], axis=0))
@@ -111,12 +111,17 @@
                         l = base + q + 2 * h + k
                         factor = jnp.where(counts_ref[l] > sub, jnp.float32(1.0), jnp.float32(0.0))
                         rows = slice(k * species, (k + 1) * species)
-                        o_ref[l] = state[h][rows] + factor * change[rows, h * points : (h + 1) * points]
+                        out_ref[l] = state[h][rows] + factor * change[rows, h * points : (h + 1) * points]
             return inner
 
-        return lax.fori_loop(0, lines // chunk, part, carry)
-
-    lax.fori_loop(0, turns_ref[0], substep, 0)
+        lax.fori_loop(0, lines // chunk, part, 0)
+
+    def two(pair, carry):
+        substep(2 * pair, o_ref, other_ref)
+        substep(2 * pair + 1, other_ref, o_ref)
+        return carry
+
+    lax.fori_loop(0, (turns_ref[0] + 1) // 2, two, 0)
 
     def pack(l, carry):
         slot = rank_ref[l]
@@ -129,7 +134,78 @@
     lax.fori_loop(0, lines, pack, 0, unroll=8)
 
 
-def land_kernel(slots, y_ref, recv_ref, aim_ref, mid_ref, o_ref, les_ref):
+def swap_kernel(names, groups, pairs, *refs):
+    sends, takes = refs[:pairs], refs[pairs : 2 * pairs]
+    send_sem, recv_sem, own_sem = refs[2 * pairs :]
+    width = lax.axis_size(names[1])
+    me = lax.axis_index(names[0]) * width + lax.axis_index(names[1])
+
+    def place(j):
+        peer = lax.rem(me + j, groups)
+        return peer, (peer // width, lax.rem(peer, width))
+
+    barrier = pltpu.get_barrier_semaphore()
+
+    def greet(j, carry):
+        pl.semaphore_signal(barrier, inc=1, device_id=place(j)[1], device_id_type=pl.DeviceIdType.MESH)
+        return carry
+
+    lax.fori_loop(1, groups, greet, 0)
+    own = [pltpu.make_async_copy(sends[p].at[me], takes[p].at[me], own_sem.at[p]) for p in range(pairs)]
+    for copy in own:
+        copy.start()
+    pl.semaphore_wait(barrier, groups - 1)
+
+    def copies(j):
+        peer, device = place(j)
+        return [
+            pltpu.make_async_remote_copy(
+                src_ref=sends[p].at[peer],
+                dst_ref=takes[p].at[me],
+                send_sem=send_sem.at[p, j],
+                recv_sem=recv_sem.at[p, j],
+                device_id=device,
+                device_id_type=pl.DeviceIdType.MESH,
+            )
+            for p in range(pairs)
+        ]
+
+    def begin(j, carry):
+        for copy in copies(j):
+            copy.start()
+        return carry
+
+    def finish(j, carry):
+        for copy in copies(j):
+            copy.wait()
+        return carry
+
+    lax.fori_loop(1, groups, begin, 0)
+    for copy in own:
+        copy.wait()
+    lax.fori_loop(1, groups, finish, 0)
+
+
+def swap(arrays, number):
+    names = ("grid", "line")
+    groups = arrays[0].shape[0]
+    pairs = len(arrays)
+    return pl.pallas_call(
+        functools.partial(swap_kernel, names, groups, pairs),
+        out_shape=[jax.ShapeDtypeStruct(a.shape, a.dtype) for a in arrays],
+        in_specs=[VMEM] * pairs,
+        out_specs=[VMEM] * pairs,
+        scratch_shapes=[
+            pltpu.SemaphoreType.DMA((pairs, groups)),
+            pltpu.SemaphoreType.DMA((pairs, groups)),
+            pltpu.SemaphoreType.DMA((pairs,)),
+        ],
+        compiler_params=pltpu.CompilerParams(collective_id=number, has_side_effects=True),
+        name="swap%d" % number,
+    )(*arrays)
+
+
+def land_kernel(step, slots, y_ref, recv_ref, aim_ref, mid_ref, o_ref, les_ref):
     lines, species, points = y_ref.shape
     groups = recv_ref.shape[0]
     segments = points // SEG
@@ -139,7 +215,7 @@
     def land(r, carry):
         got = recv_ref[r]
         for k in range(slots):
-            code = aim_ref[r * slots + k]
+            code = aim_ref[r, 0, step * slots + k]
             safe = jnp.maximum(code, 0)
             line = safe // segments
             seg = safe - line * segments
@@ -195,12 +271,11 @@
     earlier = (owner[:, :, None] == owner[:, None, :]) & (order[None, :, None] > order[None, None, :])
     rank = jnp.sum(earlier.astype(jnp.int32), axis=2)
     position = owner * slots + rank
-    code = (line_to * segments + seg_to).astype(f32)
+    code = line_to * segments + seg_to
     hit = jnp.arange(groups * slots)[None, :, None] == position[:, None, :]
-    aims = jnp.max(jnp.where(hit, code[:, None, :], -1.0), axis=2)
-    aims = aims.reshape(STEPS, groups, slots).transpose(1, 0, 2)
-    aims = lax.all_to_all(aims, ("grid", "line"), split_axis=0, concat_axis=0, tiled=True)
-    aims = aims.transpose(1, 0, 2).reshape(STEPS, groups * slots).astype(jnp.int32)
+    aims = jnp.max(jnp.where(hit, code[:, None, :], -1), axis=2)
+    aims = aims.reshape(STEPS, groups, slots).transpose(1, 0, 2).reshape(groups, 1, STEPS * slots)
+    aims = jnp.pad(aims, ((0, 0), (0, 0), (0, points - STEPS * slots)))
 
     diffuse = pl.pallas_call(
         functools.partial(diffuse_kernel, species),
@@ -217,17 +292,19 @@
         out_shape=(block, jax.ShapeDtypeStruct((groups, species, points), f32)),
         in_specs=[VMEM] * 3 + [SMEM] * 5,
         out_specs=(VMEM, VMEM),
+        scratch_shapes=[pltpu.VMEM((count, species, points), f32)],
         compiler_params=params,
         name="chem",
     )
-    land = pl.pallas_call(
-        functools.partial(land_kernel, slots),
-        out_shape=(block, jax.ShapeDtypeStruct((species, count), f32)),
-        in_specs=[VMEM, VMEM, SMEM, VMEM],
-        out_specs=(VMEM, VMEM),
-        compiler_params=params,
-        name="land",
-    )
+    def land(step, *given):
+        return pl.pallas_call(
+            functools.partial(land_kernel, step, slots),
+            out_shape=(block, jax.ShapeDtypeStruct((species, count), f32)),
+            in_specs=[VMEM, VMEM, SMEM, VMEM],
+            out_specs=(VMEM, VMEM),
+            compiler_params=params,
+            name="land",
+        )(*given)
 
     field = les
     state = lines.reshape(count, species, points)
@@ -238,8 +315,11 @@
         state, sending = chem(
             spread.reshape(count, species, points), mid, matrix, turns, counts, owner[step], rank[step], seg_from[step]
         )
-        received = lax.all_to_all(sending, ("grid", "line"), split_axis=0, concat_axis=0, tiled=True)
-        state, field = land(state, received, aims[step], mid)
+        if step == 0:
+            received, aims = swap([sending, aims], 0)
+        else:
+            (received,) = swap([sending], step)
+        state, field = land(step, state, received, aims, mid)
         field = field.reshape(les.shape)
     return (field, state.reshape(lines.shape))
 

time: 120 us -> 118 us (0.983)
  Pallas kernels: 40.9 us -> 79.6 us
  waiting for transfers between devices: 26.1 us -> 0.02 us
  starting transfers between devices: 37 us -> 18.1 us
  local copies, waits for them, and re-layouts: 7.91 us -> 12 us
    pallas_call x2 -> x4, Pallas kernels: 13 us -> 53.2 us  [the longest x2 39.2 us: swap(): pl.pallas_call(functools.partial(swap_kernel, names, groups, pairs), out_...]
    all_to_all x3 -> x0, waiting for transfers between devices: 26.1 us -> none  [the longest x2 26.1 us: body(): lax.all_to_all(sending, ('grid', 'line'), split_axis=0, concat_axis=0, ti...]
    all_to_all x3 -> x0, starting transfers between devices: 21.3 us -> none  [the longest x2 11.6 us: body(): lax.all_to_all(sending, ('grid', 'line'), split_axis=0, concat_axis=0, ti...]
    unnamed x12 -> x24, local copies, waits for them, and re-layouts: 2.58 us -> 6.77 us
    ppermute x4, starting transfers between devices: 10.6 us -> 12.9 us  [shift_along(): lax.ppermute(lax.slice_in_dim(array, length - 1, length, axis=dim), axis,...]
    pallas_call x2, Pallas kernels: 22.7 us -> 21.2 us  [body(): chem(spread.reshape(count, species, points), mid, matrix, turns, counts,...]
  transfers between devices with their start and end apart: 11 -> 8, of which waited for: 2 -> 0; matrix products, arithmetic and copies ran while one was open for 9% -> 9% of each run, Pallas kernels for 14% -> 4%
where the time goes in v2:
time: 118 us; the launch traced here: 117 us
  Pallas kernels  79.6 us (67%)
  starting transfers between devices  18.1 us (15%)
  local copies, waits for them, and re-layouts  12 us (10%)
  other arithmetic  5.32 us (5%)
    pallas_call x2, Pallas kernels, swap(): pl.pallas_call(functools.partial(swap_kernel, names, groups, pairs), out_...  39.2 us
    pallas_call x2, Pallas kernels, body(): chem(spread.reshape(count, species, points), mid, matrix, turns, counts,...  21.2 us
    pallas_call x2, Pallas kernels, land(): pl.pallas_call(functools.partial(land_kernel, step, slots), out_shape=(bl...  14.1 us
    ppermute x4, starting transfers between devices, shift_along(): lax.ppermute(lax.slice_in_dim(array, length - 1, length, axis=dim), axis,...  12.9 us
    unnamed x24, local copies, waits for them, and re-layouts  6.77 us
    ppermute x4, starting transfers between devices, shift_along(): after = lax.ppermute(lax.slice_in_dim(array, 0, 1, axis=dim), axis, down)  5.17 us
    pallas_call x2, Pallas kernels, body(): diffuse(state.reshape(count * species, points), starts[step], mixing)  5.1 us
  transfers between devices with their start and end apart: 8, of which 0 were waited for; matrix products, arithmetic and copies ran while one was open for 9% of the time, Pallas kernels for 4%

profile of v2, /device:TPU:0, one launch (start us, length us, event | category | flops | bytes accessed | tf_op | source)
XLA Modules:
  0.0 116.8 jit_solution(3877474956612531289)
XLA Ops:
  0.6 5.0 %collective-permute-start = (f32[24,1,128]{2,0,1:T(8,128)}, f32[24,1,128]{2,0,1:T(8,128)S(1)}, u32[]{:S(2)}, u32[]{:S(2)}) collective-permute-start(f32[24,1,128]{2,0,1:T(8,128)} %bitcast.58), channel_id=1, source_target_pairs={{0,8},{8,16},{16,24},{1,9},{9,17},{17,25},{2,10},{10,18},{18,26},{... | collective-permute-start | bytes 36872 | tf_op jit(solution)/shard_map/ppermute | solution.py:26
  5.6 1.3 %collective-permute-start.1 = (f32[24,1,128]{2,0,1:T(8,128)}, f32[24,1,128]{2,0,1:T(8,128)S(1)}, u32[]{:S(2)}, u32[]{:S(2)}) collective-permute-start(f32[24,1,128]{2,0,1:T(8,128)} %bitcast.59), channel_id=1, source_target_pairs={{8,0},{16,8},{24,16},{9,1},{17,9},{25,17},{10,2},{18,10},{26,18},{... | collective-permute-start | bytes 36872 | tf_op jit(solution)/shard_map/ppermute | solution.py:27
  6.9 0.9 fusion.15
  7.8 1.4 %collective-permute-start.2 = (f32[24,1,1]{2,0,1:T(8,128)S(1)}, f32[24,1,1]{2,0,1:T(8,128)S(1)}, u32[]{:S(2)}, u32[]{:S(2)}) collective-permute-start(f32[24,1,1]{2,0,1:T(8,128)S(1)} %get-tuple-element.39), channel_id=1, source_target_pairs={{0,1},{1,2},{2,3},{3,4},{4,5},{5,6},{6,7},{8,9},{9,10},{10,11},{11... | collective-permute-start | bytes 296 | tf_op jit(solution)/shard_map/ppermute | solution.py:26
  9.2 1.3 %collective-permute-start.3 = (f32[24,1,1]{2,0,1:T(8,128)S(1)}, f32[24,1,1]{2,0,1:T(8,128)S(1)}, u32[]{:S(2)}, u32[]{:S(2)}) collective-permute-start(f32[24,1,1]{2,0,1:T(8,128)S(1)} %get-tuple-element.38), channel_id=1, source_target_pairs={{1,0},{2,1},{3,2},{4,3},{5,4},{6,5},{7,6},{9,8},{10,9},{11,10},{12... | collective-permute-start | bytes 296 | tf_op jit(solution)/shard_map/ppermute | solution.py:27
  10.5 0.9 fusion.14
  11.5 0.7 slice_bitcast_fusion.2
  12.2 0.9 convert_reduce_fusion
  13.1 0.7 multiply_add_fusion.2
  13.8 0.7 multiply_divide_fusion
  14.5 0.7 slice_bitcast_fusion.3
  15.2 0.1 copy.37.start_ref
  15.3 0.8 fusion.16
  16.1 0.1 broadcast_multiply_fusion
  16.2 0.1 mul.203
  16.4 0.8 slice_bitcast_fusion
  17.1 0.1 pad_maximum_fusion.a_ref
  17.2 0.7 multiply_add_fusion.1
  17.9 0.1 select_reduce_fusion
  18.1 0.1 exponential_add_fusion.1
  18.2 1.0 multiply_add_fusion.m_ref
  19.2 2.5 %diffuse.2 = f32[3072,128]{1,0:T(8,128)S(1)} custom-call(f32[3072,128]{1,0:T(8,128)S(1)} %bitcast.50, s32[128,1]{1,0:T(8,128)S(1)} %copy.37.start_ref, f32[24,128,128]{2,1,0:T(8,128)S(1)} %multiply_add_fusion.m_ref), custom_call_target="tpu_custom_call" | custom-call | flops 301989888 | bytes 5242880 | tf_op jit(solution)/shard_map/diffuse/pallas_call | solution.py:314
  21.8 0.1 reshape.382
  22.0 0.1 copy.47
  22.0 0.1 copy.48.start_ref
  22.2 0.6 reduce_max.18
  22.8 0.6 pad.4.refs_1_
  23.4 0.1 fusion.6.mid_ref
  23.5 10.6 %chem.2 = (f32[128,24,128]{2,1,0:T(8,128)S(1)}, f32[32,24,128]{2,1,0:T(8,128)S(1)}) custom-call(f32[128,24,128]{2,1,0:T(8,128)S(1)} %bitcast.48, f32[24,128]{1,0:T(8,128)S(1)} %fusion.6.mid_ref, bf16[48,144]{1,0:T(8,128)(2,1)S(1)} %pad_maximum_fusion.a_ref, s32[1]{0:T(128)} %bitcast.12.turns_ref, s32[128]{0:T(128)S(1)} %bitcast.56, ...), custom_call_target="tpu_custom_call" | custom-call | tf_op jit(solution)/shard_map/chem/pallas_call | solution.py:315
  34.2 1.1 copy-done.2
  35.3 0.8 copy-done.5
  36.0 19.7 %swap0.1 = (f32[32,24,128]{2,1,0:T(8,128)}, s32[32,1,128]{2,1,0:T(1,128)}) custom-call(f32[32,24,128]{2,1,0:T(8,128)} %copy-done.5, s32[32,1,128]{2,1,0:T(1,128)} %pad.4.refs_1_), custom_call_target="tpu_custom_call" | custom-call | tf_op jit(solution)/shard_map/swap0/pallas_call | solution.py:193
  55.8 1.4 %copy-done.3 = f32[128,24,128]{2,1,0:T(8,128)S(1)} copy-done((f32[128,24,128]{2,1,0:T(8,128)S(1)}, f32[128,24,128]{2,1,0:T(8,128)}, u32[]{:S(2)}) %copy-start.3) | copy-done | bytes 1572888
  57.2 1.0 copy-done.7
  58.2 0.7 copy-done.8
  58.9 6.5 %land.2 = (f32[128,24,128]{2,1,0:T(8,128)S(1)}, f32[24,128]{1,0:T(8,128)S(1)}) custom-call(f32[128,24,128]{2,1,0:T(8,128)S(1)} %copy-done.3, f32[32,24,128]{2,1,0:T(8,128)S(1)} %copy-done.7, s32[32,1,128]{2,1,0:T(1,128)S(1)} %copy-done.8, f32[24,128]{1,0:T(8,128)S(1)} %fusion.6.mid_ref), custom_call_target="tpu_custom_call" | custom-call | tf_op jit(solution)/shard_map/land/pallas_call | solution.py:300
  65.4 0.1 fusion.13
  65.6 4.8 %collective-permute-start.4 = (f32[24,1,128]{2,0,1:T(8,128)S(1)}, f32[24,1,128]{2,0,1:T(8,128)S(1)}, u32[]{:S(2)}, u32[]{:S(2)}) collective-permute-start(f32[24,1,128]{2,0,1:T(8,128)S(1)} %bitcast.54), channel_id=1, source_target_pairs={{0,8},{8,16},{16,24},{1,9},{9,17},{17,25},{2,10},{10,18},{18,26},{... | collective-permute-start | bytes 36872 | tf_op jit(solution)/shard_map/ppermute | solution.py:26
  70.4 1.3 %collective-permute-start.5 = (f32[24,1,128]{2,0,1:T(8,128)S(1)}, f32[24,1,128]{2,0,1:T(8,128)S(1)}, u32[]{:S(2)}, u32[]{:S(2)}) collective-permute-start(f32[24,1,128]{2,0,1:T(8,128)S(1)} %bitcast.55), channel_id=1, source_target_pairs={{8,0},{16,8},{24,16},{9,1},{17,9},{25,17},{10,2},{18,10},{26,18},{... | collective-permute-start | bytes 36872 | tf_op jit(solution)/shard_map/ppermute | solution.py:27
  71.7 1.7 %collective-permute-start.6 = (f32[24,1,1]{2,0,1:T(8,128)S(1)}, f32[24,1,1]{2,0,1:T(8,128)S(1)}, u32[]{:S(2)}, u32[]{:S(2)}) collective-permute-start(f32[24,1,1]{2,0,1:T(8,128)S(1)} %get-tuple-element.35), channel_id=1, source_target_pairs={{0,1},{1,2},{2,3},{3,4},{4,5},{5,6},{6,7},{8,9},{9,10},{10,11},{11... | collective-permute-start | bytes 296 | tf_op jit(solution)/shard_map/ppermute | solution.py:26
  73.5 1.3 %collective-permute-start.7 = (f32[24,1,1]{2,0,1:T(8,128)S(1)}, f32[24,1,1]{2,0,1:T(8,128)S(1)}, u32[]{:S(2)}, u32[]{:S(2)}) collective-permute-start(f32[24,1,1]{2,0,1:T(8,128)S(1)} %get-tuple-element.34), channel_id=1, source_target_pairs={{1,0},{2,1},{3,2},{4,3},{5,4},{6,5},{7,6},{9,8},{10,9},{11,10},{12... | collective-permute-start | bytes 296 | tf_op jit(solution)/shard_map/ppermute | solution.py:27
  74.8 2.5 %diffuse.3 = f32[3072,128]{1,0:T(8,128)S(1)} custom-call(f32[3072,128]{1,0:T(8,128)S(1)} %bitcast.51, s32[128,1]{1,0:T(8,128)S(1)} %copy.48.start_ref, f32[24,128,128]{2,1,0:T(8,128)S(1)} %multiply_add_fusion.m_ref), custom_call_target="tpu_custom_call" | custom-call | flops 301989888 | bytes 5242880 | tf_op jit(solution)/shard_map/diffuse/pallas_call | solution.py:314
  77.4 0.1 fusion.11.mid_ref
  77.4 10.6 %chem.3 = (f32[128,24,128]{2,1,0:T(8,128)S(1)}, f32[32,24,128]{2,1,0:T(8,128)S(1)}) custom-call(f32[128,24,128]{2,1,0:T(8,128)S(1)} %bitcast.49, f32[24,128]{1,0:T(8,128)S(1)} %fusion.11.mid_ref, bf16[48,144]{1,0:T(8,128)(2,1)S(1)} %pad_maximum_fusion.a_ref, s32[1]{0:T(128)} %bitcast.12.turns_ref, s32[128]{0:T(128)S(1)} %bitcast.57, ...), custom_call_target="tpu_custom_call" | custom-call | tf_op jit(solution)/shard_map/chem/pallas_call | solution.py:315
  88.1 0.7 copy-done.6
  88.8 19.4 %swap1.1.recv_ref = f32[32,24,128]{2,1,0:T(8,128)} custom-call(f32[32,24,128]{2,1,0:T(8,128)} %copy-done.6), custom_call_target="tpu_custom_call" | custom-call | tf_op jit(solution)/shard_map/swap1/pallas_call | solution.py:193
  108.3 1.0 copy-done.4
  109.2 7.6 %land.3 = (f32[128,24,128]{2,1,0:T(8,128)}, f32[24,128]{1,0:T(8,128)}) custom-call(f32[128,24,128]{2,1,0:T(8,128)S(1)} %get-tuple-element.18.y_ref, f32[32,24,128]{2,1,0:T(8,128)S(1)} %copy-done.4, s32[32,1,128]{2,1,0:T(1,128)S(1)} %copy-done.9, f32[24,128]{1,0:T(8,128)S(1)} %fusion.11.mid_ref), custom_call_target="tpu_custom_call" | custom-call | tf_op jit(solution)/shard_map/land/pallas_call | solution.py:300
  (34 shorter events, 0.3 us)
Async XLA Ops:
  0.6 14.7 %copy-start = (f32[24,24]{1,0:T(8,128)S(1)}, f32[24,24]{1,0:T(8,128)}, u32[]{:S(2)}) copy-start(f32[24,24]{1,0:T(8,128)} %param.21) | copy-start | bytes 6916
  0.6 22.8 %collective-permute-start = (f32[24,1,128]{2,0,1:T(8,128)}, f32[24,1,128]{2,0,1:T(8,128)S(1)}, u32[]{:S(2)}, u32[]{:S(2)}) collective-permute-start(f32[24,1,128]{2,0,1:T(8,128)} %bitcast.58), channel_id=1, source_target_pairs={{0,8},{8,16},{16,24},{1,9},{9,17},{17,25},{2,10},{10,18},{18,26},{... | collective-permute-start | bytes 36872 | tf_op jit(solution)/shard_map/ppermute | solution.py:26
  5.6 17.8 %collective-permute-start.1 = (f32[24,1,128]{2,0,1:T(8,128)}, f32[24,1,128]{2,0,1:T(8,128)S(1)}, u32[]{:S(2)}, u32[]{:S(2)}) collective-permute-start(f32[24,1,128]{2,0,1:T(8,128)} %bitcast.59), channel_id=1, source_target_pairs={{8,0},{16,8},{24,16},{9,1},{17,9},{25,17},{10,2},{18,10},{26,18},{... | collective-permute-start | bytes 36872 | tf_op jit(solution)/shard_map/ppermute | solution.py:27
  7.8 15.6 %collective-permute-start.2 = (f32[24,1,1]{2,0,1:T(8,128)S(1)}, f32[24,1,1]{2,0,1:T(8,128)S(1)}, u32[]{:S(2)}, u32[]{:S(2)}) collective-permute-start(f32[24,1,1]{2,0,1:T(8,128)S(1)} %get-tuple-element.39), channel_id=1, source_target_pairs={{0,1},{1,2},{2,3},{3,4},{4,5},{5,6},{6,7},{8,9},{9,10},{10,11},{11... | collective-permute-start | bytes 296 | tf_op jit(solution)/shard_map/ppermute | solution.py:26
  9.2 14.2 %collective-permute-start.3 = (f32[24,1,1]{2,0,1:T(8,128)S(1)}, f32[24,1,1]{2,0,1:T(8,128)S(1)}, u32[]{:S(2)}, u32[]{:S(2)}) collective-permute-start(f32[24,1,1]{2,0,1:T(8,128)S(1)} %get-tuple-element.38), channel_id=1, source_target_pairs={{1,0},{2,1},{3,2},{4,3},{5,4},{6,5},{7,6},{9,8},{10,9},{11,10},{12... | collective-permute-start | bytes 296 | tf_op jit(solution)/shard_map/ppermute | solution.py:27
  16.3 2.9 %copy-start.1 = (f32[1,1,128,24,128]{4,3,2,1,0:T(8,128)S(1)}, f32[1,1,128,24,128]{4,3,2,1,0:T(8,128)}, u32[]{:S(2)}) copy-start(f32[1,1,128,24,128]{4,3,2,1,0:T(8,128)} %param.12) | copy-start | bytes 4718596
  19.2 2.9 %copy-start.10 = (s32[1,1,128]{2,1,0:T(1,128)S(1)}, s32[1,1,128]{2,1,0:T(1,128)}, u32[]{:S(2)}) copy-start(s32[1,1,128]{2,1,0:T(1,128)} %param.18) | copy-start | bytes 1540
  19.2 4.2 %copy-start.11 = (f32[24,1,128]{2,1,0:T(1,128)S(1)}, f32[24,1,128]{2,1,0:T(1,128)}, u32[]{:S(2)}) copy-start(f32[24,1,128]{2,1,0:T(1,128)} %param.11) | copy-start | bytes 36868
  34.1 1.1 copy-start.2
  35.3 0.8 copy-start.5
  55.8 1.4 %copy-start.3 = (f32[128,24,128]{2,1,0:T(8,128)S(1)}, f32[128,24,128]{2,1,0:T(8,128)}, u32[]{:S(2)}) copy-start(f32[128,24,128]{2,1,0:T(8,128)} %copy-done.2) | copy-start | bytes 4718596
  57.2 1.0 copy-start.7
  58.2 0.7 copy-start.8
  65.6 11.7 %collective-permute-start.4 = (f32[24,1,128]{2,0,1:T(8,128)S(1)}, f32[24,1,128]{2,0,1:T(8,128)S(1)}, u32[]{:S(2)}, u32[]{:S(2)}) collective-permute-start(f32[24,1,128]{2,0,1:T(8,128)S(1)} %bitcast.54), channel_id=1, source_target_pairs={{0,8},{8,16},{16,24},{1,9},{9,17},{17,25},{2,10},{10,18},{18,26},{... | collective-permute-start | bytes 36872 | tf_op jit(solution)/shard_map/ppermute | solution.py:26
  70.4 6.9 %collective-permute-start.5 = (f32[24,1,128]{2,0,1:T(8,128)S(1)}, f32[24,1,128]{2,0,1:T(8,128)S(1)}, u32[]{:S(2)}, u32[]{:S(2)}) collective-permute-start(f32[24,1,128]{2,0,1:T(8,128)S(1)} %bitcast.55), channel_id=1, source_target_pairs={{8,0},{16,8},{24,16},{9,1},{17,9},{25,17},{10,2},{18,10},{26,18},{... | collective-permute-start | bytes 36872 | tf_op jit(solution)/shard_map/ppermute | solution.py:27
  71.7 5.6 %collective-permute-start.6 = (f32[24,1,1]{2,0,1:T(8,128)S(1)}, f32[24,1,1]{2,0,1:T(8,128)S(1)}, u32[]{:S(2)}, u32[]{:S(2)}) collective-permute-start(f32[24,1,1]{2,0,1:T(8,128)S(1)} %get-tuple-element.35), channel_id=1, source_target_pairs={{0,1},{1,2},{2,3},{3,4},{4,5},{5,6},{6,7},{8,9},{9,10},{10,11},{11... | collective-permute-start | bytes 296 | tf_op jit(solution)/shard_map/ppermute | solution.py:26
  73.5 3.9 %collective-permute-start.7 = (f32[24,1,1]{2,0,1:T(8,128)S(1)}, f32[24,1,1]{2,0,1:T(8,128)S(1)}, u32[]{:S(2)}, u32[]{:S(2)}) collective-permute-start(f32[24,1,1]{2,0,1:T(8,128)S(1)} %get-tuple-element.34), channel_id=1, source_target_pairs={{1,0},{2,1},{3,2},{4,3},{5,4},{6,5},{7,6},{9,8},{10,9},{11,10},{12... | collective-permute-start | bytes 296 | tf_op jit(solution)/shard_map/ppermute | solution.py:27
  77.3 30.9 %copy-start.9 = (s32[32,1,128]{2,1,0:T(1,128)S(1)}, s32[32,1,128]{2,1,0:T(1,128)}, u32[]{:S(2)}) copy-start(s32[32,1,128]{2,1,0:T(1,128)} %get-tuple-element.15.aim_ref) | copy-start | bytes 49156
  88.1 0.7 copy-start.6
  108.2 1.0 copy-start.4
